TPU v7x, 64 devices: a 2x2x8 block of a 4x4x8 slice. The times are simulated.
64 devices in a mesh: dp: 4 (over x, y), sp: 16 (over z, core).
Axes of the slice: x: 2, y: 2, z: 8, core: 2. Of those that a mesh axis runs over, the one named last changes fastest.
The devices are a block of a 4x4x8 slice.
Arguments:
- x: bfloat16 [16384, 2560], P(('dp', 'sp')), parts along dimension 0
- g_kv: bfloat16 [2560], replicated
- w_k: bfloat16 [2560, 20, 128], replicated
- w_v: bfloat16 [2560, 20, 128], replicated
- g_attn: bfloat16 [2, 2560], replicated
- w_q: bfloat16 [2, 2560, 20, 128], replicated
- w_o: bfloat16 [2, 20, 128, 2560], replicated
- g_mlp: bfloat16 [2, 2560], replicated
- w_gate: bfloat16 [2, 2560, 6912], replicated
- w_up: bfloat16 [2, 2560, 6912], replicated
- w_down: bfloat16 [2, 6912, 2560], replicated
Outputs:
- output: bfloat16 [16384, 2560], P(('dp', 'sp')), parts along dimension 0
There are 4 independent parts. A program takes and returns all parts, laid end to end along the dimension named above; an argument that names none is the same for every part.
All inputs are finite; a program needn't handle non-finite values.
Results may differ from a plain program's by a relative error of at most 0.0103382.
Values are sent between devices in bfloat16 or wider.
A program may use at most 768 MiB of HBM per device.

v0:
```python
import math
import jax
import jax.numpy as jnp
from jax import lax
from jax.sharding import PartitionSpec as P

EPS = 1e-6


def rms_norm(act_rows, gain_vec):
    act_f32 = act_rows.astype(jnp.float32)
    inv_rms = lax.rsqrt(jnp.mean(act_f32 * act_f32, axis=-1, keepdims=True) + EPS)
    return (act_f32 * inv_rms * gain_vec.astype(jnp.float32)).astype(jnp.bfloat16)


def attend_local(queries, key_rows, value_rows, shard_start):
    tokens, num_heads, head_dim = queries.shape
    q_block = math.gcd(tokens, 64)
    score_scale = head_dim ** -0.5
    key_pos = jnp.arange(key_rows.shape[0])

    def one_block(block_idx):
        start_row = block_idx * q_block
        q_rows = lax.dynamic_slice_in_dim(queries, start_row, q_block, axis=0)
        scores = jnp.einsum("qhe,khe->hqk", q_rows, key_rows, preferred_element_type=jnp.float32) * score_scale
        query_pos = shard_start + start_row + jnp.arange(q_block)
        causal_mask = key_pos[None, :] <= query_pos[:, None]
        scores = jnp.where(causal_mask[None], scores, -jnp.inf)
        attn_probs = jax.nn.softmax(scores, axis=-1).astype(jnp.bfloat16)
        return jnp.einsum("hqk,khe->qhe", attn_probs, value_rows, preferred_element_type=jnp.float32).astype(jnp.bfloat16)

    blocks = lax.map(one_block, jnp.arange(tokens // q_block))
    return blocks.reshape(tokens, num_heads, head_dim)


def solution(mesh):
    row_spec = P(("dp", "sp"), None)
    in_specs = (row_spec,) + (P(),) * 10

    def local_block(x_rows, g_kv, w_k, w_v, g_attn, w_q, w_o, g_mlp, w_gate, w_up, w_down):
        tokens = x_rows.shape[0]
        shard_start = lax.axis_index("sp") * tokens
        normed = rms_norm(x_rows, g_kv)
        key_local = jnp.einsum("td,dhe->the", normed, w_k, preferred_element_type=jnp.float32).astype(jnp.bfloat16)
        value_local = jnp.einsum("td,dhe->the", normed, w_v, preferred_element_type=jnp.float32).astype(jnp.bfloat16)
        key_rows = lax.all_gather(key_local, "sp", axis=0, tiled=True)
        value_rows = lax.all_gather(value_local, "sp", axis=0, tiled=True)
        hidden = x_rows
        for layer_idx in range(w_q.shape[0]):
            normed_a = rms_norm(hidden, g_attn[layer_idx])
            queries = jnp.einsum("td,dhe->the", normed_a, w_q[layer_idx], preferred_element_type=jnp.float32).astype(jnp.bfloat16)
            attn_rows = attend_local(queries, key_rows, value_rows, shard_start)
            attn_out = jnp.einsum("the,hed->td", attn_rows, w_o[layer_idx], preferred_element_type=jnp.float32)
            hidden = (hidden.astype(jnp.float32) + attn_out).astype(jnp.bfloat16)
            normed_m = rms_norm(hidden, g_mlp[layer_idx])
            gate_act = jnp.dot(normed_m, w_gate[layer_idx], preferred_element_type=jnp.float32)
            up_act = jnp.dot(normed_m, w_up[layer_idx], preferred_element_type=jnp.float32)
            mixed = (jax.nn.silu(gate_act) * up_act).astype(jnp.bfloat16)
            mlp_out = jnp.dot(mixed, w_down[layer_idx], preferred_element_type=jnp.float32)
            hidden = (hidden.astype(jnp.float32) + mlp_out).astype(jnp.bfloat16)
        return hidden

    return jax.shard_map(local_block, mesh=mesh, in_specs=in_specs, out_specs=row_spec, check_vma=False)
```

profile of v0, /device:TPU:21, one launch (start us, length us, event | category | flops | bytes accessed | tf_op | source)
XLA Modules:
  0.0 679.2 jit_solution(11890918607081557619)
XLA Ops:
  39.2 96.6 %all-gather.3.cloned.1.call-done = bf16[4096,20,128]{2,0,1:T(8,128)(2,1)} async-done(((bf16[256,20,128]{2,0,1:T(8,128)(2,1)}), bf16[4096,20,128]{2,0,1:T(8,128)(2,1)}) %all-gather.3.cloned.1.call-update) | async-done | bytes 20971536 | tf_op jit(solution)/shard_map/all_gather | solution.py:46
  135.8 112.0 %all-gather.5.cloned.1.call-done = bf16[4096,20,128]{2,0,1:T(8,128)(2,1)} async-done(((bf16[256,20,128]{2,0,1:T(8,128)(2,1)}), bf16[4096,20,128]{2,0,1:T(8,128)(2,1)}) %all-gather.5.cloned.1.call-update) | async-done | bytes 20971536 | tf_op jit(solution)/shard_map/all_gather | solution.py:47
  248.1 148.6 %while.22 = (s32[]{:T(128)}, bf16[4,64,20,128]{3,1,0,2:T(8,128)(2,1)S(1)}, s32[4]{0:T(128)S(1)}, s32[]{:T(128)}, bf16[256,20,128]{2,0,1:T(8,128)(2,1)}, /*index=...) while((s32[]{:T(128)}, ...), condition=%wide.region_4.5_spmd.clone, body=%wide.region_1.4_spmd.clone.sunk | while | flops 2716241920 | bytes 85083840 | solution.py:32
  249.7 20.6 %fusion.194 = (f32[20,64]{1,0:T(8,128)S(1)}, f32[20,64,4096]{2,1,0:T(8,128)}) fusion(pred[64,4096]{1,0:T(8,128)(4,1)S(1)} %iota_compare_fusion.4, bf16[4096,20,128]{2,0,1:T(8,128)(2,1)} %get-tuple-element.286, bf16[256,20,128]{2,0,1:T(8,128)(2,1)} %get-tuple-element.285, s32[]{:T(128)S(6)} %select_n.42), kind=kOutput, calls=%fused_computation.131.clone.1 | convolution fusion | flops 1363152896 | bytes 42537988 | tf_op jit(solution)/shard_map/while/body/eval_jaxpr/sub | solution.py:29
  270.3 15.1 %fusion.195 = bf16[4,64,20,128]{3,1,0,2:T(8,128)(2,1)S(1)} fusion(bf16[4,64,20,128]{3,1,0,2:T(8,128)(2,1)S(1)} %get-tuple-element.271, s32[]{:T(128)} %get-tuple-element.270, bf16[4096,20,128]{2,0,1:T(8,128)(2,1)} %get-tuple-element.287, f32[20,64,4096]{2,1,0:T(8,128)} %get-tuple-element.248, f32[20,64]{1,0:T(8,128)S(1)} %get-tuple-element.249), kind=kOutput, calls=%fused_computation.14.clone.1 | convolution fusion | flops 1352826880 | bytes 42283012 | tf_op jit(solution)/shard_map/while/body/eval_jaxpr/hqk,khe->qhe/dot_general | solution.py:30
  286.8 20.6 %fusion.194 = (f32[20,64]{1,0:T(8,128)S(1)}, f32[20,64,4096]{2,1,0:T(8,128)}) fusion(pred[64,4096]{1,0:T(8,128)(4,1)S(1)} %iota_compare_fusion.4, bf16[4096,20,128]{2,0,1:T(8,128)(2,1)} %get-tuple-element.286, bf16[256,20,128]{2,0,1:T(8,128)(2,1)} %get-tuple-element.285, s32[]{:T(128)S(6)} %select_n.42), kind=kOutput, calls=%fused_computation.131.clone.1 | convolution fusion | flops 1363152896 | bytes 42537988 | tf_op jit(solution)/shard_map/while/body/eval_jaxpr/sub | solution.py:29
  307.4 15.1 %fusion.195 = bf16[4,64,20,128]{3,1,0,2:T(8,128)(2,1)S(1)} fusion(bf16[4,64,20,128]{3,1,0,2:T(8,128)(2,1)S(1)} %get-tuple-element.271, s32[]{:T(128)} %get-tuple-element.270, bf16[4096,20,128]{2,0,1:T(8,128)(2,1)} %get-tuple-element.287, f32[20,64,4096]{2,1,0:T(8,128)} %get-tuple-element.248, f32[20,64]{1,0:T(8,128)S(1)} %get-tuple-element.249), kind=kOutput, calls=%fused_computation.14.clone.1 | convolution fusion | flops 1352826880 | bytes 42283012 | tf_op jit(solution)/shard_map/while/body/eval_jaxpr/hqk,khe->qhe/dot_general | solution.py:30
  323.9 20.6 %fusion.194 = (f32[20,64]{1,0:T(8,128)S(1)}, f32[20,64,4096]{2,1,0:T(8,128)}) fusion(pred[64,4096]{1,0:T(8,128)(4,1)S(1)} %iota_compare_fusion.4, bf16[4096,20,128]{2,0,1:T(8,128)(2,1)} %get-tuple-element.286, bf16[256,20,128]{2,0,1:T(8,128)(2,1)} %get-tuple-element.285, s32[]{:T(128)S(6)} %select_n.42), kind=kOutput, calls=%fused_computation.131.clone.1 | convolution fusion | flops 1363152896 | bytes 42537988 | tf_op jit(solution)/shard_map/while/body/eval_jaxpr/sub | solution.py:29
  344.5 15.1 %fusion.195 = bf16[4,64,20,128]{3,1,0,2:T(8,128)(2,1)S(1)} fusion(bf16[4,64,20,128]{3,1,0,2:T(8,128)(2,1)S(1)} %get-tuple-element.271, s32[]{:T(128)} %get-tuple-element.270, bf16[4096,20,128]{2,0,1:T(8,128)(2,1)} %get-tuple-element.287, f32[20,64,4096]{2,1,0:T(8,128)} %get-tuple-element.248, f32[20,64]{1,0:T(8,128)S(1)} %get-tuple-element.249), kind=kOutput, calls=%fused_computation.14.clone.1 | convolution fusion | flops 1352826880 | bytes 42283012 | tf_op jit(solution)/shard_map/while/body/eval_jaxpr/hqk,khe->qhe/dot_general | solution.py:30
  361.0 20.6 %fusion.194 = (f32[20,64]{1,0:T(8,128)S(1)}, f32[20,64,4096]{2,1,0:T(8,128)}) fusion(pred[64,4096]{1,0:T(8,128)(4,1)S(1)} %iota_compare_fusion.4, bf16[4096,20,128]{2,0,1:T(8,128)(2,1)} %get-tuple-element.286, bf16[256,20,128]{2,0,1:T(8,128)(2,1)} %get-tuple-element.285, s32[]{:T(128)S(6)} %select_n.42), kind=kOutput, calls=%fused_computation.131.clone.1 | convolution fusion | flops 1363152896 | bytes 42537988 | tf_op jit(solution)/shard_map/while/body/eval_jaxpr/sub | solution.py:29
  381.6 15.1 %fusion.195 = bf16[4,64,20,128]{3,1,0,2:T(8,128)(2,1)S(1)} fusion(bf16[4,64,20,128]{3,1,0,2:T(8,128)(2,1)S(1)} %get-tuple-element.271, s32[]{:T(128)} %get-tuple-element.270, bf16[4096,20,128]{2,0,1:T(8,128)(2,1)} %get-tuple-element.287, f32[20,64,4096]{2,1,0:T(8,128)} %get-tuple-element.248, f32[20,64]{1,0:T(8,128)S(1)} %get-tuple-element.249), kind=kOutput, calls=%fused_computation.14.clone.1 | convolution fusion | flops 1352826880 | bytes 42283012 | tf_op jit(solution)/shard_map/while/body/eval_jaxpr/hqk,khe->qhe/dot_general | solution.py:30
  404.6 15.3 %fusion.62 = f32[256,6912]{1,0:T(8,128)S(1)} fusion(bf16[2,2560,6912]{2,1,0:T(8,128)(2,1)} %param.23, bf16[256,2560]{1,0:T(8,128)(2,1)S(1)} %get-tuple-element.160, f32[2560]{0:T(1024)S(1)} %copy-done.6, f32[256]{0:T(256)S(1)} %add_rsqrt_fusion.2), kind=kOutput, calls=%fused_computation.56 | convolution fusion | flops 9062318080 | bytes 43789312 | tf_op jit(solution)/shard_map/dot_general | solution.py:56
  419.9 17.8 %fusion.91 = bf16[256,6912]{1,0:T(8,128)(2,1)} fusion(bf16[2,2560,6912]{2,1,0:T(8,128)(2,1)} %param.24, f32[256,6912]{1,0:T(8,128)S(1)} %fusion.62, bf16[256,2560]{1,0:T(8,128)(2,1)} %copy-done.8, f32[2560]{0:T(1024)S(1)} %copy-done.6, f32[256]{0:T(256)S(1)} %add_rsqrt_fusion.2), kind=kOutput, calls=%fused_computation.79 | convolution fusion | flops 9072934912 | bytes 47328256 | tf_op jit(solution)/shard_map/dot_general | solution.py:57
  437.7 17.4 %fusion.132 = (f32[256]{0:T(256)S(1)}, bf16[256,2560]{1,0:T(8,128)(2,1)S(1)}) fusion(bf16[256,6912]{1,0:T(8,128)(2,1)} %fusion.91, bf16[2,6912,2560]{2,1,0:T(8,128)(2,1)} %param.25, bf16[256,2560]{1,0:T(8,128)(2,1)} %copy-done.8), kind=kOutput, calls=%fused_computation.106 | convolution fusion | flops 9063628800 | bytes 41550848 | tf_op jit(solution)/shard_map/dot_general | solution.py:59
  464.3 148.0 %while.23 = (s32[]{:T(128)}, bf16[4,64,20,128]{3,1,0,2:T(8,128)(2,1)S(1)}, s32[4]{0:T(128)S(1)}, s32[]{:T(128)}, bf16[256,20,128]{2,0,1:T(8,128)(2,1)S(1)}, /*in...) while((s32[]{:T(128)}, ...), condition=%wide.region_10.11_spmd.clone, body=%wide.region_7.10_spmd.clone.sunk | while | flops 2716241920 | bytes 85083840 | solution.py:32
  465.8 20.4 %fusion.199 = (f32[20,64]{1,0:T(8,128)S(1)}, f32[20,64,4096]{2,1,0:T(8,128)}) fusion(pred[64,4096]{1,0:T(8,128)(4,1)S(1)} %iota_compare_fusion.5, bf16[4096,20,128]{2,0,1:T(8,128)(2,1)} %get-tuple-element.319, bf16[256,20,128]{2,0,1:T(8,128)(2,1)S(1)} %get-tuple-element.318, s32[]{:T(128)S(6)} %select_n.44), kind=kOutput, calls=%fused_computation.132.clone.1 | convolution fusion | flops 1363152896 | bytes 42537988 | tf_op jit(solution)/shard_map/while/body/eval_jaxpr/sub | solution.py:29
  502.8 20.4 %fusion.199 = (f32[20,64]{1,0:T(8,128)S(1)}, f32[20,64,4096]{2,1,0:T(8,128)}) fusion(pred[64,4096]{1,0:T(8,128)(4,1)S(1)} %iota_compare_fusion.5, bf16[4096,20,128]{2,0,1:T(8,128)(2,1)} %get-tuple-element.319, bf16[256,20,128]{2,0,1:T(8,128)(2,1)S(1)} %get-tuple-element.318, s32[]{:T(128)S(6)} %select_n.44), kind=kOutput, calls=%fused_computation.132.clone.1 | convolution fusion | flops 1363152896 | bytes 42537988 | tf_op jit(solution)/shard_map/while/body/eval_jaxpr/sub | solution.py:29
  539.8 20.4 %fusion.199 = (f32[20,64]{1,0:T(8,128)S(1)}, f32[20,64,4096]{2,1,0:T(8,128)}) fusion(pred[64,4096]{1,0:T(8,128)(4,1)S(1)} %iota_compare_fusion.5, bf16[4096,20,128]{2,0,1:T(8,128)(2,1)} %get-tuple-element.319, bf16[256,20,128]{2,0,1:T(8,128)(2,1)S(1)} %get-tuple-element.318, s32[]{:T(128)S(6)} %select_n.44), kind=kOutput, calls=%fused_computation.132.clone.1 | convolution fusion | flops 1363152896 | bytes 42537988 | tf_op jit(solution)/shard_map/while/body/eval_jaxpr/sub | solution.py:29
  560.2 15.1 %fusion.200 = bf16[4,64,20,128]{3,1,0,2:T(8,128)(2,1)S(1)} fusion(bf16[4,64,20,128]{3,1,0,2:T(8,128)(2,1)S(1)} %get-tuple-element.304, s32[]{:T(128)} %get-tuple-element.303, bf16[4096,20,128]{2,0,1:T(8,128)(2,1)} %get-tuple-element.320, f32[20,64,4096]{2,1,0:T(8,128)} %get-tuple-element.257, f32[20,64]{1,0:T(8,128)S(1)} %get-tuple-element.258), kind=kOutput, calls=%fused_computation.36.clone.1 | convolution fusion | flops 1352826880 | bytes 42283012 | tf_op jit(solution)/shard_map/while/body/eval_jaxpr/hqk,khe->qhe/dot_general | solution.py:30
  576.8 20.4 %fusion.199 = (f32[20,64]{1,0:T(8,128)S(1)}, f32[20,64,4096]{2,1,0:T(8,128)}) fusion(pred[64,4096]{1,0:T(8,128)(4,1)S(1)} %iota_compare_fusion.5, bf16[4096,20,128]{2,0,1:T(8,128)(2,1)} %get-tuple-element.319, bf16[256,20,128]{2,0,1:T(8,128)(2,1)S(1)} %get-tuple-element.318, s32[]{:T(128)S(6)} %select_n.44), kind=kOutput, calls=%fused_computation.132.clone.1 | convolution fusion | flops 1363152896 | bytes 42537988 | tf_op jit(solution)/shard_map/while/body/eval_jaxpr/sub | solution.py:29
  597.2 15.1 %fusion.200 = bf16[4,64,20,128]{3,1,0,2:T(8,128)(2,1)S(1)} fusion(bf16[4,64,20,128]{3,1,0,2:T(8,128)(2,1)S(1)} %get-tuple-element.304, s32[]{:T(128)} %get-tuple-element.303, bf16[4096,20,128]{2,0,1:T(8,128)(2,1)} %get-tuple-element.320, f32[20,64,4096]{2,1,0:T(8,128)} %get-tuple-element.257, f32[20,64]{1,0:T(8,128)S(1)} %get-tuple-element.258), kind=kOutput, calls=%fused_computation.36.clone.1 | convolution fusion | flops 1352826880 | bytes 42283012 | tf_op jit(solution)/shard_map/while/body/eval_jaxpr/hqk,khe->qhe/dot_general | solution.py:30
  620.7 15.3 %fusion.56 = f32[256,6912]{1,0:T(8,128)S(1)} fusion(bf16[2,2560,6912]{2,1,0:T(8,128)(2,1)} %param.23, bf16[256,2560]{1,0:T(8,128)(2,1)S(1)} %get-tuple-element.164, f32[2560]{0:T(1024)S(1)} %copy-done.4, f32[256]{0:T(256)S(1)} %add_rsqrt_fusion), kind=kOutput, calls=%fused_computation.50 | convolution fusion | flops 9062318080 | bytes 43789312 | tf_op jit(solution)/shard_map/dot_general | solution.py:56
  636.0 17.8 %fusion.88 = bf16[256,6912]{1,0:T(8,128)(2,1)} fusion(bf16[2,2560,6912]{2,1,0:T(8,128)(2,1)} %param.24, f32[256,6912]{1,0:T(8,128)S(1)} %fusion.56, bf16[256,2560]{1,0:T(8,128)(2,1)} %copy-done.9, f32[2560]{0:T(1024)S(1)} %copy-done.4, f32[256]{0:T(256)S(1)} %add_rsqrt_fusion), kind=kOutput, calls=%fused_computation.78 | convolution fusion | flops 9072934912 | bytes 47328256 | tf_op jit(solution)/shard_map/dot_general | solution.py:57
  653.8 18.1 %fusion.112 = bf16[256,2560]{1,0:T(8,128)(2,1)} fusion(bf16[256,6912]{1,0:T(8,128)(2,1)} %fusion.88, bf16[2,6912,2560]{2,1,0:T(8,128)(2,1)} %param.25, bf16[256,2560]{1,0:T(8,128)(2,1)} %copy-done.9), kind=kOutput, calls=%fused_computation.94 | convolution fusion | flops 9061662720 | bytes 41549824 | tf_op jit(solution)/shard_map/dot_general | solution.py:59
  (68 shorter events, 94.9 us)
Async XLA Ops:
  6.5 129.3 %all-gather.3.cloned.1.call-start = ((), (), s32[]{:S(2)}) async-start(), calls=%async_computation | async-start | bytes 22282240 | tf_op jit(solution)/shard_map/all_gather | solution.py:46
  8.9 10.1 %copy-start = (bf16[256,2560]{1,0:T(8,128)(2,1)S(1)}, bf16[256,2560]{1,0:T(8,128)(2,1)}, u32[]{:S(2)}) copy-start(bf16[256,2560]{1,0:T(8,128)(2,1)} %param.15) | copy-start | bytes 3932164
  18.9 9.6 %copy-start.2 = (bf16[2,2560]{1,0:T(2,128)(2,1)S(1)}, bf16[2,2560]{1,0:T(2,128)(2,1)}, u32[]{:S(2)}) copy-start(bf16[2,2560]{1,0:T(2,128)(2,1)} %param.19) | copy-start | bytes 30724
  18.9 10.3 %copy-start.3 = (bf16[2,2560]{1,0:T(2,128)(2,1)S(1)}, bf16[2,2560]{1,0:T(2,128)(2,1)}, u32[]{:S(2)}) copy-start(bf16[2,2560]{1,0:T(2,128)(2,1)} %param.22) | copy-start | bytes 30724
  18.9 228.9 %all-gather.5.cloned.1.call-start = ((), (), s32[]{:S(2)}) async-start(), calls=%async_computation.1 | async-start | bytes 22282240 | tf_op jit(solution)/shard_map/all_gather | solution.py:47
  248.1 148.6 %copy-start.1 = (bf16[256,2560]{1,0:T(8,128)(2,1)S(1)}, bf16[256,2560]{1,0:T(8,128)(2,1)}, u32[]{:S(2)}) copy-start(bf16[256,2560]{1,0:T(8,128)(2,1)} %param.15) | copy-start | bytes 3932164
  396.7 7.9 %copy-start.6 = (f32[2560]{0:T(1024)S(1)}, f32[2560]{0:T(1024)}, u32[]{:S(2)}) copy-start(f32[2560]{0:T(1024)} %get-tuple-element.124) | copy-start | bytes 30724
  403.6 1.1 copy-start.8
  437.7 17.4 %copy-start.5 = (f32[2560]{0:T(1024)S(1)}, f32[2560]{0:T(1024)}, u32[]{:S(2)}) copy-start(f32[2560]{0:T(1024)} %get-tuple-element.125) | copy-start | bytes 30724
  455.2 8.8 %copy-start.7 = (bf16[256,2560]{1,0:T(8,128)(2,1)}, bf16[256,2560]{1,0:T(8,128)(2,1)S(1)}, u32[]{:S(2)}) copy-start(bf16[256,2560]{1,0:T(8,128)(2,1)S(1)} %get-tuple-element.162) | copy-start | bytes 3932164
  612.3 8.3 %copy-start.4 = (f32[2560]{0:T(1024)S(1)}, f32[2560]{0:T(1024)}, u32[]{:S(2)}) copy-start(f32[2560]{0:T(1024)} %get-tuple-element.123) | copy-start | bytes 30724
  619.6 1.1 copy-start.9
Sparse Core Ops, SparseCore 0:
  19.0 116.7 all-gather.2
  137.5 110.2 all-gather.4
where the time goes:
time: 686 us; the launch traced here: 679 us
  matrix products  438 us (64%)
  waiting for transfers between devices  209 us (30%)
  between operations  14.1 us (2%)
  local copies, waits for them, and re-layouts  7.54 us (1%)
    sub x8, matrix products, one_block(): attn_probs = jax.nn.softmax(scores, axis=-1).astype(jnp.bfloat16)  164 us
    dot_general x8, matrix products, one_block(): jnp.einsum('hqk,khe->qhe', attn_probs, value_rows, preferred_element_type...  121 us
    all_gather x1, waiting for transfers between devices, local_block(): value_rows = lax.all_gather(value_local, 'sp', axis=0, tiled=True)  112 us
    all_gather x1, waiting for transfers between devices, local_block(): key_rows = lax.all_gather(key_local, 'sp', axis=0, tiled=True)  96.6 us
    dot_general x2, matrix products, local_block(): jnp.dot(normed_m, w_up[layer_idx], preferred_element_type=jnp.float32)  35.6 us
    dot_general x2, matrix products, local_block(): jnp.dot(mixed, w_down[layer_idx], preferred_element_type=jnp.float32)  35.5 us
    dot_general x2, matrix products, local_block(): jnp.dot(normed_m, w_gate[layer_idx], preferred_element_type=jnp.float32)  30.6 us
    dot_general x2, matrix products, local_block(): jnp.einsum('td,dhe->the', normed_a, w_q[layer_idx], preferred_element_typ...  18.2 us
  transfers between devices with their start and end apart: 2, of which 2 were waited for; matrix products, arithmetic and copies ran while one was open for 3% of the time, Pallas kernels for 0%

commit v1 on v0

v1 whole, which is shorter than its diff:
```python
import functools
import math

import jax
import jax.numpy as jnp
from jax import lax
from jax.experimental import pallas as pl
from jax.experimental.pallas import tpu as pltpu
from jax.sharding import PartitionSpec as P

EPS = 1e-6
LOG2E = 1.4426950408889634
MESH = pl.DeviceIdType.MESH
VMEM_LIMIT = 67043328
GROUP = 4


def norm_rows(src, gain, dst):
    rows = src.shape[0]
    step = math.gcd(rows, 32)
    g = gain[...].astype(jnp.float32)

    @pl.loop(0, rows // step)
    def _(i):
        sl = pl.ds(pl.multiple_of(i * step, step), step)
        v = src[sl, :].astype(jnp.float32)
        inv = lax.rsqrt(jnp.mean(v * v, axis=-1, keepdims=True) + EPS)
        dst[sl, :] = (v * inv * g).astype(jnp.bfloat16)


def heads_matrix(w):
    return jnp.concatenate([w[i] for i in range(GROUP)], axis=1)


def project(n, w):
    return jnp.dot(n, heads_matrix(w), preferred_element_type=jnp.float32).astype(jnp.bfloat16)


def attend_block(k_ref, v_ref, q_ref, m_ref, l_ref, acc_ref, unroll, mask=None):
    heads, _, head_dim = k_ref.shape
    scale = LOG2E * head_dim ** -0.5

    @pl.loop(0, heads // unroll)
    def _(g):
        hs = [g * unroll + i for i in range(unroll)]
        scores = [
            jnp.dot(k_ref[h], q_ref[h], preferred_element_type=jnp.float32) * scale
            for h in hs
        ]
        if mask is not None:
            scores = [jnp.where(mask, s, -jnp.inf) for s in scores]
        for h, s in zip(hs, scores):
            m_old = m_ref[h]
            m_new = jnp.maximum(m_old, jnp.max(s, axis=0, keepdims=True))
            alpha = jnp.exp2(m_old - m_new)
            p = jnp.exp2(s - m_new)
            m_ref[h] = m_new
            l_ref[h] = l_ref[h] * alpha + jnp.sum(p, axis=0, keepdims=True)
            acc_ref[h] = acc_ref[h] * alpha + jnp.dot(
                v_ref[h], p.astype(jnp.bfloat16), preferred_element_type=jnp.float32
            )


def reset_state(m_ref, l_ref, acc_ref):
    m_ref[...] = jnp.full_like(m_ref, -jnp.inf)
    l_ref[...] = jnp.zeros_like(l_ref)

    @pl.loop(0, acc_ref.shape[0])
    def _(h):
        acc_ref[h] = jnp.zeros(acc_ref.shape[1:], jnp.float32)


def write_attention(o_ref, l_ref, acc_ref):
    heads, head_dim, _ = acc_ref.shape

    for h in range(heads):
        o = acc_ref[h] / l_ref[h]
        o_ref[:, h * head_dim:(h + 1) * head_dim] = o.T.astype(jnp.bfloat16)


def causal_mask(tokens, half, core, d):
    shape = (2 * half, tokens)
    k = lax.broadcasted_iota(jnp.int32, shape, 0)
    q = lax.broadcasted_iota(jnp.int32, shape, 1)
    key_pos = jnp.where(k >= half, k - half + tokens, k) + d * half
    return key_pos <= q + core * tokens


def unit_valid(u, d, chip, chips):
    s = (u + 1) // 2
    return (chip >= s) if d == 0 else (chip + s >= chips)


def gather_attend_kernel(
    n_sp, x_hbm, g_kv, g_q, wk_hbm, wv_hbm, wq_hbm,
    k_all, v_all, o_ref,
    wk, wv, wq, xs, nb, kb, vb, ka, va, qt, m_ref, l_ref, acc,
    x_sem, w_sem, q_sem, send_sem, recv_sem, st_sem, px_sem, pr_sem, ld_sem,
):
    heads, depth, head_dim = wk.shape
    tokens = nb.shape[0]
    half = tokens // 2
    groups = heads // GROUP
    chips = n_sp // 2
    me = lax.axis_index("sp")
    chip = me // 2
    core = me - 2 * chip
    right = lax.rem(me + 2, n_sp)
    left = lax.rem(me + n_sp - 2, n_sp)
    partner = me + 1 - 2 * core

    barrier = pltpu.get_barrier_semaphore()
    for dev in (left, right, partner):
        pl.semaphore_signal(barrier, inc=1, device_id={"sp": dev}, device_id_type=MESH)
    pl.semaphore_wait(barrier, 3)

    def hop(src, u, d):
        return pltpu.make_async_remote_copy(
            src_ref=src,
            dst_ref=xs.at[u, pl.ds(d * half, half), :],
            send_sem=send_sem.at[u, d],
            recv_sem=recv_sem.at[u, d],
            device_id={"sp": right if d == 0 else left},
            device_id_type=MESH,
        )

    def own(u, d):
        return hop(x_hbm.at[pl.ds((u - 1) * half, half), :], u, d)

    def relay(u_from, u, d):
        return hop(xs.at[u_from, pl.ds(d * half, half), :], u, d)

    for u in (1, 2):
        for d in (0, 1):
            own(u, d).start()
    x_copy = pltpu.make_async_copy(x_hbm, xs.at[0], x_sem)
    x_copy.start()

    def w_copy(which, j):
        src, dst = ((wk_hbm, wk), (wv_hbm, wv))[which]
        sl = pl.ds(j * GROUP, GROUP)
        return pltpu.make_async_copy(src.at[sl], dst.at[sl], w_sem.at[which, j])

    def q_copy(j, slot):
        return pltpu.make_async_copy(
            wq_hbm.at[0, pl.ds(j * GROUP, GROUP)], wq.at[slot], q_sem.at[slot])

    for j in range(groups):
        w_copy(0, j).start()
        w_copy(1, j).start()
    for j in range(min(2, groups)):
        q_copy(j, j).start()
    reset_state(m_ref, l_ref, acc)
    x_copy.wait()

    def stores(u, slot):
        out = []
        for i, (buf, full) in enumerate(((kb, k_all), (vb, v_all))):
            for d in (0, 1):
                part = pl.ds(d * half, half)
                mine = pl.ds(core * half, half)
                if i == 0:
                    src, dst = buf.at[slot, :, part, :], full.at[u, d, :, mine, :]
                else:
                    src, dst = buf.at[slot, :, :, part], full.at[u, d, :, :, mine]
                local = pltpu.make_async_copy(src, dst, st_sem.at[slot, i, d])
                remote = pltpu.make_async_remote_copy(
                    src_ref=src, dst_ref=dst,
                    send_sem=px_sem.at[slot, i, d], recv_sem=pr_sem.at[u, i, d],
                    device_id={"sp": partner}, device_id_type=MESH,
                )
                out.append((local, remote))
        return out

    def loads(u, d):
        return (
            pltpu.make_async_copy(k_all.at[u, d], ka.at[d], ld_sem.at[d, 0]),
            pltpu.make_async_copy(v_all.at[u, d], va.at[d], ld_sem.at[d, 1]),
        )

    def finish_stores(u):
        for local, remote in stores(u, lax.rem(u, 2)):
            local.wait()
            remote.wait_send()
            remote.wait_recv()

    def attend_unit(u):
        for d in (0, 1):
            for copy in loads(u, d):
                copy.wait()

            @pl.when(unit_valid(u, d, chip, chips))
            def _():
                attend_block(ka.at[d], va.at[d], qt, m_ref, l_ref, acc, 4)

    def attend_own():
        for d in (0, 1):
            for copy in loads(0, d):
                copy.wait()
            attend_block(ka.at[d], va.at[d], qt, m_ref, l_ref, acc, 2,
                         mask=causal_mask(tokens, half, core, d))

    @pl.loop(0, chips)
    def _(u):
        slot = lax.rem(u, 2)

        @pl.when(u >= 1)
        def _():
            for d in (0, 1):
                relay(0, u, d).wait_recv()

        @pl.when(jnp.logical_and(u >= 1, u <= chips - 4))
        def _():
            for d in (0, 1):
                relay(u, u + 2, d).start()

        @pl.when(u == chips - 3)
        def _():
            relay(u, u + 2, 0).start()

        @pl.when(u == chips - 2)
        def _():
            relay(u, u + 1, 1).start()

        @pl.when(u >= 1)
        def _():
            finish_stores(u - 1)
            for d in (0, 1):
                for copy in loads(u - 1, d):
                    copy.start()

        norm_rows(xs.at[u], g_kv, nb)

        @pl.loop(0, groups)
        def _(j):
            @pl.when(u == 0)
            def _():
                w_copy(0, j).wait()
                w_copy(1, j).wait()

            sl = pl.ds(j * GROUP, GROUP)
            n = nb[...]
            k = project(n, wk[sl])
            v = project(n, wv[sl])
            for i in range(GROUP):
                cols = slice(i * head_dim, (i + 1) * head_dim)
                kb[slot, j * GROUP + i] = k[:, cols]
                vb[slot, j * GROUP + i] = v[:, cols].T

        for local, remote in stores(u, slot):
            local.start()
            remote.start()

        @pl.when(u == 0)
        def _():
            norm_rows(xs.at[0], g_q, nb)

            @pl.loop(0, groups)
            def _(j):
                qslot = lax.rem(j, 2)
                q_copy(j, qslot).wait()
                q = project(nb[...], wq[qslot])
                for i in range(GROUP):
                    qt[j * GROUP + i] = q[:, i * head_dim:(i + 1) * head_dim].T

                @pl.when(j + 2 < groups)
                def _():
                    q_copy(j + 2, qslot).start()

        @pl.when(u == 1)
        def _():
            attend_own()

        @pl.when(u >= 2)
        def _():
            attend_unit(u - 1)

    last = chips - 1
    finish_stores(last)
    for d in (0, 1):
        for copy in loads(last, d):
            copy.start()
    attend_unit(last)
    write_attention(o_ref, l_ref, acc)
    for u in range(1, chips):
        for d in (0, 1):
            relay(0, u, d).wait_send()


def gather_attend(n_sp, x, g_kv, g_q, wk, wv, wq):
    tokens, depth = x.shape
    heads, _, head_dim = wk.shape
    chips = n_sp // 2
    bf, f32 = jnp.bfloat16, jnp.float32
    dma = pltpu.SemaphoreType.DMA
    groups = heads // GROUP
    any_spec = pl.BlockSpec(memory_space=pl.ANY)
    vmem = pl.BlockSpec(memory_space=pltpu.VMEM)
    return pl.pallas_call(
        functools.partial(gather_attend_kernel, n_sp),
        out_shape=(
            jax.ShapeDtypeStruct((chips, 2, heads, tokens, head_dim), bf),
            jax.ShapeDtypeStruct((chips, 2, heads, head_dim, tokens), bf),
            jax.ShapeDtypeStruct((tokens, heads * head_dim), bf),
        ),
        in_specs=[any_spec, vmem, vmem, any_spec, any_spec, any_spec],
        out_specs=(any_spec, any_spec, vmem),
        scratch_shapes=[
            pltpu.VMEM((heads, depth, head_dim), bf),
            pltpu.VMEM((heads, depth, head_dim), bf),
            pltpu.VMEM((2, GROUP, depth, head_dim), bf),
            pltpu.VMEM((chips, tokens, depth), bf),
            pltpu.VMEM((tokens, depth), bf),
            pltpu.VMEM((2, heads, tokens, head_dim), bf),
            pltpu.VMEM((2, heads, head_dim, tokens), bf),
            pltpu.VMEM((2, heads, tokens, head_dim), bf),
            pltpu.VMEM((2, heads, head_dim, tokens), bf),
            pltpu.VMEM((heads, head_dim, tokens), bf),
            pltpu.VMEM((heads, 1, tokens), f32),
            pltpu.VMEM((heads, 1, tokens), f32),
            pltpu.VMEM((heads, head_dim, tokens), f32),
            dma,
            dma((2, groups)),
            dma((2,)),
            dma((chips, 2)),
            dma((chips, 2)),
            dma((2, 2, 2)),
            dma((2, 2, 2)),
            dma((chips, 2, 2)),
            dma((2, 2)),
        ],
        compiler_params=pltpu.CompilerParams(
            collective_id=0, has_side_effects=True, vmem_limit_bytes=VMEM_LIMIT
        ),
        name="gather_attend",
    )(x, g_kv, g_q, wk, wv, wq)


def attend_kernel(
    n_sp, layer, h_ref, g_q, wq_hbm, k_all, v_all, o_ref,
    wq, nb, ka, va, qt, m_ref, l_ref, acc, q_sem, ld_sem,
):
    heads, head_dim, tokens = qt.shape
    half = tokens // 2
    groups = heads // GROUP
    chips = n_sp // 2
    bufs = ka.shape[0]
    me = lax.axis_index("sp")
    chip = me // 2
    core = me - 2 * chip

    def q_copy(j, slot):
        return pltpu.make_async_copy(
            wq_hbm.at[layer, pl.ds(j * GROUP, GROUP)], wq.at[slot], q_sem.at[slot])

    def loads(u, d, slot):
        return (
            pltpu.make_async_copy(k_all.at[u, d], ka.at[slot], ld_sem.at[slot, 0]),
            pltpu.make_async_copy(v_all.at[u, d], va.at[slot], ld_sem.at[slot, 1]),
        )

    for j in range(min(2, groups)):
        q_copy(j, j).start()
    for i in range(bufs):
        for copy in loads(i // 2, i % 2, i):
            copy.start()
    reset_state(m_ref, l_ref, acc)
    norm_rows(h_ref, g_q, nb)

    @pl.loop(0, groups)
    def _(j):
        qslot = lax.rem(j, 2)
        q_copy(j, qslot).wait()
        q = project(nb[...], wq[qslot])
        for i in range(GROUP):
            qt[j * GROUP + i] = q[:, i * head_dim:(i + 1) * head_dim].T

        @pl.when(j + 2 < groups)
        def _():
            q_copy(j + 2, qslot).start()

    @pl.loop(0, chips)
    def _(u):
        for d in (0, 1):
            slot = lax.rem(2 * u + d, bufs)
            for copy in loads(u, d, slot):
                copy.wait()

            @pl.when(u == 0)
            def _():
                attend_block(ka.at[slot], va.at[slot], qt, m_ref, l_ref, acc, 2,
                             mask=causal_mask(tokens, half, core, d))

            @pl.when(jnp.logical_and(u > 0, unit_valid(u, d, chip, chips)))
            def _():
                attend_block(ka.at[slot], va.at[slot], qt, m_ref, l_ref, acc, 4)

            nxt = 2 * u + d + bufs

            @pl.when(nxt < 2 * chips)
            def _():
                for copy in loads(nxt // 2, lax.rem(nxt, 2), slot):
                    copy.start()

    write_attention(o_ref, l_ref, acc)


def attend(n_sp, layer, h, g_q, wq, k_all, v_all):
    tokens, depth = h.shape
    _, heads, _, head_dim = wq.shape
    bf, f32 = jnp.bfloat16, jnp.float32
    dma = pltpu.SemaphoreType.DMA
    bufs = 4
    any_spec = pl.BlockSpec(memory_space=pl.ANY)
    vmem = pl.BlockSpec(memory_space=pltpu.VMEM)
    return pl.pallas_call(
        functools.partial(attend_kernel, n_sp, layer),
        out_shape=jax.ShapeDtypeStruct((tokens, heads * head_dim), bf),
        in_specs=[vmem, vmem, any_spec, any_spec, any_spec],
        out_specs=vmem,
        scratch_shapes=[
            pltpu.VMEM((2, GROUP, depth, head_dim), bf),
            pltpu.VMEM((tokens, depth), bf),
            pltpu.VMEM((bufs, heads, tokens, head_dim), bf),
            pltpu.VMEM((bufs, heads, head_dim, tokens), bf),
            pltpu.VMEM((heads, head_dim, tokens), bf),
            pltpu.VMEM((heads, 1, tokens), f32),
            pltpu.VMEM((heads, 1, tokens), f32),
            pltpu.VMEM((heads, head_dim, tokens), f32),
            dma((2,)),
            dma((bufs, 2)),
        ],
        compiler_params=pltpu.CompilerParams(vmem_limit_bytes=VMEM_LIMIT),
        name="attend",
    )(h, g_q, wq, k_all, v_all)


def tail_kernel(
    layer, o_ref, h_ref, g_ref, wo_hbm, wg_hbm, wu_hbm, wd_hbm, out_ref,
    wo, wg, wu, wd, hm, nb, acc, mb, o_sem, w_sem,
):
    tokens, depth = h_ref.shape
    parts, _, o_cols = wo.shape
    bufs, _, cols = wg.shape
    steps = wg_hbm.shape[2] // cols
    sub = math.gcd(cols, 256)
    span = math.gcd(depth, 512)

    def o_copy(j):
        return pltpu.make_async_copy(
            wo_hbm.at[layer, :, pl.ds(j * o_cols, o_cols)], wo.at[j], o_sem.at[j])

    def w_copies(i, slot):
        sl = pl.ds(pl.multiple_of(i * cols, cols), cols)
        return (
            pltpu.make_async_copy(wg_hbm.at[layer, :, sl], wg.at[slot], w_sem.at[slot, 0]),
            pltpu.make_async_copy(wu_hbm.at[layer, :, sl], wu.at[slot], w_sem.at[slot, 1]),
            pltpu.make_async_copy(wd_hbm.at[layer, sl, :], wd.at[slot], w_sem.at[slot, 2]),
        )

    for j in range(parts):
        o_copy(j).start()
    for i in range(min(bufs, steps)):
        for copy in w_copies(i, i):
            copy.start()

    for j in range(parts):
        o_copy(j).wait()
        sl = slice(j * o_cols, (j + 1) * o_cols)
        r = jnp.dot(o_ref[...], wo[j], preferred_element_type=jnp.float32)
        h = (h_ref[:, sl].astype(jnp.float32) + r).astype(jnp.bfloat16)
        hm[:, sl] = h
        acc[:, sl] = h.astype(jnp.float32)
    norm_rows(hm, g_ref, nb)

    @pl.loop(0, steps)
    def _(i):
        slot = lax.rem(i, bufs)
        for copy in w_copies(i, slot):
            copy.wait()
        n = nb[...]
        for s in range(cols // sub):
            sl = slice(s * sub, (s + 1) * sub)
            a = jnp.dot(n, wg[slot, :, sl], preferred_element_type=jnp.float32)
            b = jnp.dot(n, wu[slot, :, sl], preferred_element_type=jnp.float32)
            mb[:, sl] = (jax.nn.silu(a) * b).astype(jnp.bfloat16)
        m = mb[...]
        for t in range(depth // span):
            sl = slice(t * span, (t + 1) * span)
            acc[:, sl] += jnp.dot(m, wd[slot, :, sl], preferred_element_type=jnp.float32)

        @pl.when(i + bufs < steps)
        def _():
            for copy in w_copies(i + bufs, slot):
                copy.start()

    out_ref[...] = acc[...].astype(jnp.bfloat16)


def tail(layer, o, h, g, wo, wg, wu, wd):
    tokens, depth = h.shape
    ff = wg.shape[2]
    bf, f32 = jnp.bfloat16, jnp.float32
    dma = pltpu.SemaphoreType.DMA
    bufs = 3
    cols = math.gcd(ff, 768)
    o_cols = math.gcd(depth, 512)
    parts = depth // o_cols
    any_spec = pl.BlockSpec(memory_space=pl.ANY)
    vmem = pl.BlockSpec(memory_space=pltpu.VMEM)
    return pl.pallas_call(
        functools.partial(tail_kernel, layer),
        out_shape=jax.ShapeDtypeStruct((tokens, depth), bf),
        in_specs=[vmem, vmem, vmem] + [any_spec] * 4,
        out_specs=vmem,
        scratch_shapes=[
            pltpu.VMEM((parts, wo.shape[1], o_cols), bf),
            pltpu.VMEM((bufs, depth, cols), bf),
            pltpu.VMEM((bufs, depth, cols), bf),
            pltpu.VMEM((bufs, cols, depth), bf),
            pltpu.VMEM((tokens, depth), bf),
            pltpu.VMEM((tokens, depth), bf),
            pltpu.VMEM((tokens, depth), f32),
            pltpu.VMEM((tokens, cols), bf),
            dma((parts,)),
            dma((bufs, 3)),
        ],
        compiler_params=pltpu.CompilerParams(vmem_limit_bytes=VMEM_LIMIT),
        name="tail",
    )(o, h, g, wo, wg, wu, wd)


def solution(mesh):
    n_sp = mesh.shape["sp"]
    row_spec = P(("dp", "sp"), None)
    in_specs = (row_spec,) + (P(),) * 10

    def local_block(x, g_kv, w_k, w_v, g_attn, w_q, w_o, g_mlp, w_gate, w_up, w_down):
        depth = x.shape[1]
        wk = w_k.transpose(1, 0, 2)
        wv = w_v.transpose(1, 0, 2)
        wq = w_q.transpose(0, 2, 1, 3)
        wo = w_o.reshape(w_o.shape[0], -1, depth)
        k_all, v_all, o = gather_attend(
            n_sp, x, g_kv.reshape(1, -1), g_attn[0:1], wk, wv, wq)
        h = tail(0, o, x, g_mlp[0:1], wo, w_gate, w_up, w_down)
        for layer in range(1, w_q.shape[0]):
            o = attend(n_sp, layer, h, g_attn[layer:layer + 1], wq, k_all, v_all)
            h = tail(layer, o, h, g_mlp[layer:layer + 1], wo, w_gate, w_up, w_down)
        return h

    return jax.shard_map(local_block, mesh=mesh, in_specs=in_specs, out_specs=row_spec, check_vma=False)
```

time: 686 us -> 319 us (0.47)
  the two profiles are of different devices: /device:TPU:21 before, /device:TPU:254 now
where the time goes in v1:
time: 319 us; the launch traced here: 318 us
  Pallas kernels  314 us (98%)
  local copies, waits for them, and re-layouts  4.09 us (1%)
    pallas_call x1, Pallas kernels, gather_attend(): pl.pallas_call(functools.partial(gather_attend_kernel, n_sp), out_shape=(...  151 us
    pallas_call x2, Pallas kernels, tail(): pl.pallas_call(functools.partial(tail_kernel, layer), out_shape=jax.Shape...  96 us
    pallas_call x1, Pallas kernels, attend(): pl.pallas_call(functools.partial(attend_kernel, n_sp, layer), out_shape=j...  67.4 us

profile of v1, /device:TPU:254, one launch (start us, length us, event | category | flops | bytes accessed | tf_op | source)
XLA Modules:
  0.0 318.4 jit_solution(16057024673136417069)
XLA Ops:
  0.0 1.3 reshape.6.g_kv
  1.3 1.4 fusion.1
  2.7 1.4 fusion
  4.1 150.7 %gather_attend.1 = (bf16[8,2,20,256,128]{4,3,2,1,0:T(8,128)(2,1)}, bf16[8,2,20,128,256]{4,3,2,1,0:T(8,128)(2,1)}, bf16[256,2560]{1,0:T(8,128)(2,1)}) custom-call(bf16[256,2560]{1,0:T(8,128)(2,1)} %h_ref.1, bf16[1,2560]{1,0:T(2,128)(2,1)} %reshape.6.g_kv, bf16[1,2560]{1,0:T(2,128)(2,1)} %get-tuple-element.14.g_q, bf16[20,2560,128]{2,1,0:T(8,128)(2,1)} %bitcast.8, ...), custom_call_target="tpu_custom_call" | custom-call | tf_op jit(solution)/shard_map/gather_attend/pallas_call | solution.py:299
  154.8 48.1 %tail.2.h_ref = bf16[256,2560]{1,0:T(8,128)(2,1)} custom-call(bf16[256,2560]{1,0:T(8,128)(2,1)} %get-tuple-element.8.o_ref, bf16[256,2560]{1,0:T(8,128)(2,1)} %h_ref.1, bf16[1,2560]{1,0:T(2,128)(2,1)} %get-tuple-element.12.g_ref, bf16[2,2560,2560]{2,1,0:T(8,128)(2,1)} %bitcast.4, bf16[2,2560,6912]{2,1,0:T(8,128)(2,1)} %wg_hbm.3, ...), custom_call_target="tpu_custom_call" | custom-call | tf_op jit(solution)/shard_map/tail/pallas_call | solution.py:511
  202.9 67.4 %attend.1.o_ref = bf16[256,2560]{1,0:T(8,128)(2,1)} custom-call(bf16[256,2560]{1,0:T(8,128)(2,1)} %tail.2.h_ref, bf16[1,2560]{1,0:T(2,128)(2,1)} %get-tuple-element.13.g_q, bf16[2,20,2560,128]{3,2,1,0:T(8,128)(2,1)} %bitcast.7, bf16[8,2,20,256,128]{4,3,2,1,0:T(8,128)(2,1)} %get-tuple-element.9.k_all, bf16[8,2,20,128,256]{4,3,2,1,0:T(8,128)(2,1)} %get-tuple-element.10.v_all), custom_call_target="tpu_custom_call" | custom-call | tf_op jit(solution)/shard_map/attend/pallas_call | solution.py:416
  270.3 47.9 %tail.3 = bf16[256,2560]{1,0:T(8,128)(2,1)} custom-call(bf16[256,2560]{1,0:T(8,128)(2,1)} %attend.1.o_ref, bf16[256,2560]{1,0:T(8,128)(2,1)} %tail.2.h_ref, bf16[1,2560]{1,0:T(2,128)(2,1)} %get-tuple-element.11.g_ref, bf16[2,2560,2560]{2,1,0:T(8,128)(2,1)} %bitcast.5, bf16[2,2560,6912]{2,1,0:T(8,128)(2,1)} %wg_hbm.3, bf16[2,2560,6912]{2,1,0:T(8,128)(2,1)} %wu_hbm.3, ...), custom_call_target="tpu_custom_call" | custom-call | tf_op jit(solution)/shard_map/tail/pallas_call | solution.py:511

commit v2 on v1

--- a/solution.py
+++ b/solution.py
@@ -13,19 +13,22 @@
 MESH = pl.DeviceIdType.MESH
 VMEM_LIMIT = 67043328
 GROUP = 4
+UNROLL = 4
 
 
 def norm_rows(src, gain, dst):
     rows = src.shape[0]
-    step = math.gcd(rows, 32)
-    g = gain[...].astype(jnp.float32)
-
-    @pl.loop(0, rows // step)
-    def _(i):
+    step = math.gcd(rows, 16)
+    g = gain.astype(jnp.float32)
+
+    def body(i, carry):
         sl = pl.ds(pl.multiple_of(i * step, step), step)
         v = src[sl, :].astype(jnp.float32)
         inv = lax.rsqrt(jnp.mean(v * v, axis=-1, keepdims=True) + EPS)
         dst[sl, :] = (v * inv * g).astype(jnp.bfloat16)
+        return carry
+
+    lax.fori_loop(0, rows // step, body, 0, unroll=4)
 
 
 def heads_matrix(w):
@@ -36,29 +39,54 @@
     return jnp.dot(n, heads_matrix(w), preferred_element_type=jnp.float32).astype(jnp.bfloat16)
 
 
-def attend_block(k_ref, v_ref, q_ref, m_ref, l_ref, acc_ref, unroll, mask=None):
-    heads, _, head_dim = k_ref.shape
+def all_sublanes(x, op):
+    for shift in (4, 2, 1):
+        x = op(x, pltpu.roll(x, shift, 0))
+    return x
+
+
+def attend_block(ks, vs, q_ref, m_ref, l_ref, acc_ref, s_refs, masks=None):
+    heads, size, head_dim = ks[0].shape
+    tokens = q_ref.shape[2]
     scale = LOG2E * head_dim ** -0.5
-
-    @pl.loop(0, heads // unroll)
-    def _(g):
-        hs = [g * unroll + i for i in range(unroll)]
-        scores = [
-            jnp.dot(k_ref[h], q_ref[h], preferred_element_type=jnp.float32) * scale
-            for h in hs
-        ]
-        if mask is not None:
-            scores = [jnp.where(mask, s, -jnp.inf) for s in scores]
-        for h, s in zip(hs, scores):
-            m_old = m_ref[h]
-            m_new = jnp.maximum(m_old, jnp.max(s, axis=0, keepdims=True))
-            alpha = jnp.exp2(m_old - m_new)
-            p = jnp.exp2(s - m_new)
-            m_ref[h] = m_new
-            l_ref[h] = l_ref[h] * alpha + jnp.sum(p, axis=0, keepdims=True)
-            acc_ref[h] = acc_ref[h] * alpha + jnp.dot(
-                v_ref[h], p.astype(jnp.bfloat16), preferred_element_type=jnp.float32
-            )
+    n = size // 8
+
+    def scores(h, s_ref):
+        top = None
+        for i, k in enumerate(ks):
+            s = jnp.dot(k[h], q_ref[h], preferred_element_type=jnp.float32)
+            if masks is not None:
+                s = jnp.where(masks[i], s, -jnp.inf)
+            s = s.reshape(n, 8, tokens)
+            s_ref[i * n:(i + 1) * n] = s
+            t = jnp.max(s, axis=0)
+            top = t if top is None else jnp.maximum(top, t)
+        return all_sublanes(top, jnp.maximum)
+
+    def update(h, s_ref, top):
+        m_old = m_ref[h]
+        m_new = jnp.maximum(m_old, top * scale)
+        alpha = jnp.exp2(m_old - m_new)
+        m_ref[h] = m_new
+        p = jnp.exp2(s_ref[:n * len(ks)] * scale - m_new[None])
+        l_ref[h] = l_ref[h] * alpha + jnp.sum(p, axis=0)
+        p = p.reshape(size * len(ks), tokens).astype(jnp.bfloat16)
+        v = jnp.concatenate([r[h] for r in vs], axis=1) if len(vs) > 1 else vs[0][h]
+        o = jnp.dot(v, p, preferred_element_type=jnp.float32)
+        acc_ref[h] = acc_ref[h] * alpha[None] + o.reshape(head_dim // 8, 8, tokens)
+
+    def body(g, top):
+        h = UNROLL * g
+        for i in range(UNROLL):
+            nxt = h + i + 1
+            if i == UNROLL - 1:
+                nxt = jnp.minimum(nxt, heads - 1)
+            after = scores(nxt, s_refs[(i + 1) % 2])
+            update(h + i, s_refs[i % 2], top)
+            top = after
+        return top
+
+    lax.fori_loop(0, heads // UNROLL, body, scores(0, s_refs[0]))
 
 
 def reset_state(m_ref, l_ref, acc_ref):
@@ -71,11 +99,15 @@
 
 
 def write_attention(o_ref, l_ref, acc_ref):
-    heads, head_dim, _ = acc_ref.shape
-
-    for h in range(heads):
-        o = acc_ref[h] / l_ref[h]
-        o_ref[:, h * head_dim:(h + 1) * head_dim] = o.T.astype(jnp.bfloat16)
+    heads, _, _, tokens = acc_ref.shape
+    head_dim = o_ref.shape[1] // heads
+
+    @pl.loop(0, heads)
+    def _(h):
+        inv = 1.0 / all_sublanes(l_ref[h], jnp.add)
+        o = (acc_ref[h] * inv[None]).reshape(head_dim, tokens)
+        cols = pl.ds(pl.multiple_of(h * head_dim, head_dim), head_dim)
+        o_ref[:, cols] = o.astype(jnp.bfloat16).T
 
 
 def causal_mask(tokens, half, core, d):
@@ -86,15 +118,22 @@
     return key_pos <= q + core * tokens
 
 
-def unit_valid(u, d, chip, chips):
+def attend_valid(u, chip, chips, ks, vs, state):
     s = (u + 1) // 2
-    return (chip >= s) if d == 0 else (chip + s >= chips)
+
+    @pl.when(chip + s >= chips)
+    def _():
+        attend_block(ks, vs, *state)
+
+    @pl.when(jnp.logical_and(chip >= s, chip + s < chips))
+    def _():
+        attend_block(ks[:1], vs[:1], *state)
 
 
 def gather_attend_kernel(
     n_sp, x_hbm, g_kv, g_q, wk_hbm, wv_hbm, wq_hbm,
     k_all, v_all, o_ref,
-    wk, wv, wq, xs, nb, kb, vb, ka, va, qt, m_ref, l_ref, acc,
+    wk, wv, wq, xs, nb, kb, vb, ka, va, qt, m_ref, l_ref, acc, s0, s1,
     x_sem, w_sem, q_sem, send_sem, recv_sem, st_sem, px_sem, pr_sem, ld_sem,
 ):
     heads, depth, head_dim = wk.shape
@@ -145,60 +184,60 @@
         return pltpu.make_async_copy(
             wq_hbm.at[0, pl.ds(j * GROUP, GROUP)], wq.at[slot], q_sem.at[slot])
 
-    for j in range(groups):
+    ahead = min(2, groups)
+    for j in range(ahead):
         w_copy(0, j).start()
         w_copy(1, j).start()
-    for j in range(min(2, groups)):
-        q_copy(j, j).start()
     reset_state(m_ref, l_ref, acc)
     x_copy.wait()
 
-    def stores(u, slot):
+    def stores(u, slot, j):
         out = []
+        hs = pl.ds(j * GROUP, GROUP)
         for i, (buf, full) in enumerate(((kb, k_all), (vb, v_all))):
             for d in (0, 1):
                 part = pl.ds(d * half, half)
                 mine = pl.ds(core * half, half)
                 if i == 0:
-                    src, dst = buf.at[slot, :, part, :], full.at[u, d, :, mine, :]
+                    src, dst = buf.at[slot, hs, part, :], full.at[u, d, hs, mine, :]
                 else:
-                    src, dst = buf.at[slot, :, :, part], full.at[u, d, :, :, mine]
-                local = pltpu.make_async_copy(src, dst, st_sem.at[slot, i, d])
+                    src, dst = buf.at[slot, hs, :, part], full.at[u, d, hs, :, mine]
+                local = pltpu.make_async_copy(src, dst, st_sem.at[slot, j, i, d])
                 remote = pltpu.make_async_remote_copy(
                     src_ref=src, dst_ref=dst,
-                    send_sem=px_sem.at[slot, i, d], recv_sem=pr_sem.at[u, i, d],
+                    send_sem=px_sem.at[slot, j, i, d], recv_sem=pr_sem.at[u, j, i, d],
                     device_id={"sp": partner}, device_id_type=MESH,
                 )
                 out.append((local, remote))
         return out
 
-    def loads(u, d):
-        return (
-            pltpu.make_async_copy(k_all.at[u, d], ka.at[d], ld_sem.at[d, 0]),
-            pltpu.make_async_copy(v_all.at[u, d], va.at[d], ld_sem.at[d, 1]),
-        )
+    def loads(u):
+        out = []
+        for d in (0, 1):
+            out.append(pltpu.make_async_copy(k_all.at[u, d], ka.at[d], ld_sem.at[d, 0]))
+            out.append(pltpu.make_async_copy(v_all.at[u, d], va.at[d], ld_sem.at[d, 1]))
+        return out
 
     def finish_stores(u):
-        for local, remote in stores(u, lax.rem(u, 2)):
-            local.wait()
-            remote.wait_send()
-            remote.wait_recv()
+        @pl.loop(0, groups)
+        def _(j):
+            for local, remote in stores(u, lax.rem(u, 2), j):
+                local.wait()
+                remote.wait_send()
+                remote.wait_recv()
+
+    state = (qt, m_ref, l_ref, acc, (s0, s1))
 
     def attend_unit(u):
-        for d in (0, 1):
-            for copy in loads(u, d):
-                copy.wait()
-
-            @pl.when(unit_valid(u, d, chip, chips))
-            def _():
-                attend_block(ka.at[d], va.at[d], qt, m_ref, l_ref, acc, 4)
+        for copy in loads(u):
+            copy.wait()
+        attend_valid(u, chip, chips, [ka.at[0], ka.at[1]], [va.at[0], va.at[1]], state)
 
     def attend_own():
-        for d in (0, 1):
-            for copy in loads(0, d):
-                copy.wait()
-            attend_block(ka.at[d], va.at[d], qt, m_ref, l_ref, acc, 2,
-                         mask=causal_mask(tokens, half, core, d))
+        for copy in loads(0):
+            copy.wait()
+        masks = [causal_mask(tokens, half, core, d) for d in (0, 1)]
+        attend_block([ka.at[0], ka.at[1]], [va.at[0], va.at[1]], *state, masks=masks)
 
     @pl.loop(0, chips)
     def _(u):
@@ -225,11 +264,10 @@
         @pl.when(u >= 1)
         def _():
             finish_stores(u - 1)
-            for d in (0, 1):
-                for copy in loads(u - 1, d):
-                    copy.start()
-
-        norm_rows(xs.at[u], g_kv, nb)
+            for copy in loads(u - 1):
+                copy.start()
+
+        norm_rows(xs.at[u], g_kv[...].reshape(1, depth), nb)
 
         @pl.loop(0, groups)
         def _(j):
@@ -237,6 +275,15 @@
             def _():
                 w_copy(0, j).wait()
                 w_copy(1, j).wait()
+
+                @pl.when(j + ahead < groups)
+                def _():
+                    w_copy(0, j + ahead).start()
+                    w_copy(1, j + ahead).start()
+
+                @pl.when(j + ahead >= groups)
+                def _():
+                    q_copy(j + ahead - groups, j + ahead - groups).start()
 
             sl = pl.ds(j * GROUP, GROUP)
             n = nb[...]
@@ -246,14 +293,13 @@
                 cols = slice(i * head_dim, (i + 1) * head_dim)
                 kb[slot, j * GROUP + i] = k[:, cols]
                 vb[slot, j * GROUP + i] = v[:, cols].T
-
-        for local, remote in stores(u, slot):
-            local.start()
-            remote.start()
+            for local, remote in stores(u, slot, j):
+                local.start()
+                remote.start()
 
         @pl.when(u == 0)
         def _():
-            norm_rows(xs.at[0], g_q, nb)
+            norm_rows(xs.at[0], g_q[0:1, :], nb)
 
             @pl.loop(0, groups)
             def _(j):
@@ -277,9 +323,8 @@
 
     last = chips - 1
     finish_stores(last)
-    for d in (0, 1):
-        for copy in loads(last, d):
-            copy.start()
+    for copy in loads(last):
+        copy.start()
     attend_unit(last)
     write_attention(o_ref, l_ref, acc)
     for u in range(1, chips):
@@ -316,17 +361,19 @@
             pltpu.VMEM((2, heads, tokens, head_dim), bf),
             pltpu.VMEM((2, heads, head_dim, tokens), bf),
             pltpu.VMEM((heads, head_dim, tokens), bf),
-            pltpu.VMEM((heads, 1, tokens), f32),
-            pltpu.VMEM((heads, 1, tokens), f32),
-            pltpu.VMEM((heads, head_dim, tokens), f32),
+            pltpu.VMEM((heads, 8, tokens), f32),
+            pltpu.VMEM((heads, 8, tokens), f32),
+            pltpu.VMEM((heads, head_dim // 8, 8, tokens), f32),
+            pltpu.VMEM((tokens // 4, 8, tokens), f32),
+            pltpu.VMEM((tokens // 4, 8, tokens), f32),
             dma,
             dma((2, groups)),
             dma((2,)),
             dma((chips, 2)),
             dma((chips, 2)),
-            dma((2, 2, 2)),
-            dma((2, 2, 2)),
-            dma((chips, 2, 2)),
+            dma((2, groups, 2, 2)),
+            dma((2, groups, 2, 2)),
+            dma((chips, groups, 2, 2)),
             dma((2, 2)),
         ],
         compiler_params=pltpu.CompilerParams(
@@ -338,13 +385,14 @@
 
 def attend_kernel(
     n_sp, layer, h_ref, g_q, wq_hbm, k_all, v_all, o_ref,
-    wq, nb, ka, va, qt, m_ref, l_ref, acc, q_sem, ld_sem,
+    wq, nb, ka, va, qt, m_ref, l_ref, acc, s0, s1, q_sem, ld_sem,
 ):
     heads, head_dim, tokens = qt.shape
     half = tokens // 2
     groups = heads // GROUP
     chips = n_sp // 2
     bufs = ka.shape[0]
+    q_bufs = wq.shape[0]
     me = lax.axis_index("sp")
     chip = me // 2
     core = me - 2 * chip
@@ -353,54 +401,65 @@
         return pltpu.make_async_copy(
             wq_hbm.at[layer, pl.ds(j * GROUP, GROUP)], wq.at[slot], q_sem.at[slot])
 
-    def loads(u, d, slot):
+    def loads(u, slot):
         return (
-            pltpu.make_async_copy(k_all.at[u, d], ka.at[slot], ld_sem.at[slot, 0]),
-            pltpu.make_async_copy(v_all.at[u, d], va.at[slot], ld_sem.at[slot, 1]),
+            pltpu.make_async_copy(k_all.at[u], ka.at[slot], ld_sem.at[slot, 0]),
+            pltpu.make_async_copy(v_all.at[u], va.at[slot], ld_sem.at[slot, 1]),
         )
 
-    for j in range(min(2, groups)):
+    for j in range(min(q_bufs, groups)):
         q_copy(j, j).start()
-    for i in range(bufs):
-        for copy in loads(i // 2, i % 2, i):
-            copy.start()
     reset_state(m_ref, l_ref, acc)
-    norm_rows(h_ref, g_q, nb)
+    norm_rows(h_ref, g_q[layer:layer + 1, :], nb)
 
     @pl.loop(0, groups)
     def _(j):
-        qslot = lax.rem(j, 2)
+        qslot = lax.rem(j, q_bufs)
         q_copy(j, qslot).wait()
+
+        @pl.when(j >= groups - min(bufs - 1, groups))
+        def _():
+            i = j - (groups - min(bufs - 1, groups))
+            for copy in loads(i, i):
+                copy.start()
+
         q = project(nb[...], wq[qslot])
         for i in range(GROUP):
             qt[j * GROUP + i] = q[:, i * head_dim:(i + 1) * head_dim].T
 
-        @pl.when(j + 2 < groups)
-        def _():
-            q_copy(j + 2, qslot).start()
+        @pl.when(j + q_bufs < groups)
+        def _():
+            q_copy(j + q_bufs, qslot).start()
+
+    for i in range(min(bufs - 1, groups), bufs - 1):
+        for copy in loads(i, i):
+            copy.start()
+
+    state = (qt, m_ref, l_ref, acc, (s0, s1))
 
     @pl.loop(0, chips)
     def _(u):
-        for d in (0, 1):
-            slot = lax.rem(2 * u + d, bufs)
-            for copy in loads(u, d, slot):
-                copy.wait()
-
-            @pl.when(u == 0)
-            def _():
-                attend_block(ka.at[slot], va.at[slot], qt, m_ref, l_ref, acc, 2,
-                             mask=causal_mask(tokens, half, core, d))
-
-            @pl.when(jnp.logical_and(u > 0, unit_valid(u, d, chip, chips)))
-            def _():
-                attend_block(ka.at[slot], va.at[slot], qt, m_ref, l_ref, acc, 4)
-
-            nxt = 2 * u + d + bufs
-
-            @pl.when(nxt < 2 * chips)
-            def _():
-                for copy in loads(nxt // 2, lax.rem(nxt, 2), slot):
-                    copy.start()
+        slot = lax.rem(u, bufs)
+        for copy in loads(u, slot):
+            copy.wait()
+        ahead = u + bufs - 1
+
+        @pl.when(ahead < chips)
+        def _():
+            for copy in loads(ahead, lax.rem(ahead, bufs)):
+                copy.start()
+
+        ks = [ka.at[slot, d] for d in (0, 1)]
+        vs = [va.at[slot, d] for d in (0, 1)]
+
+        @pl.when(u == 0)
+        def _():
+            masks = [causal_mask(tokens, half, core, d) for d in (0, 1)]
+            attend_block(ks, vs, *state, masks=masks)
+
+        @pl.when(u > 0)
+        def _():
+            attend_valid(u, chip, chips, ks, vs, state)
 
     write_attention(o_ref, l_ref, acc)
 
@@ -410,7 +469,7 @@
     _, heads, _, head_dim = wq.shape
     bf, f32 = jnp.bfloat16, jnp.float32
     dma = pltpu.SemaphoreType.DMA
-    bufs = 4
+    bufs = 3
     any_spec = pl.BlockSpec(memory_space=pl.ANY)
     vmem = pl.BlockSpec(memory_space=pltpu.VMEM)
     return pl.pallas_call(
@@ -419,15 +478,17 @@
         in_specs=[vmem, vmem, any_spec, any_spec, any_spec],
         out_specs=vmem,
         scratch_shapes=[
-            pltpu.VMEM((2, GROUP, depth, head_dim), bf),
+            pltpu.VMEM((3, GROUP, depth, head_dim), bf),
             pltpu.VMEM((tokens, depth), bf),
-            pltpu.VMEM((bufs, heads, tokens, head_dim), bf),
-            pltpu.VMEM((bufs, heads, head_dim, tokens), bf),
+            pltpu.VMEM((bufs, 2, heads, tokens, head_dim), bf),
+            pltpu.VMEM((bufs, 2, heads, head_dim, tokens), bf),
             pltpu.VMEM((heads, head_dim, tokens), bf),
-            pltpu.VMEM((heads, 1, tokens), f32),
-            pltpu.VMEM((heads, 1, tokens), f32),
-            pltpu.VMEM((heads, head_dim, tokens), f32),
-            dma((2,)),
+            pltpu.VMEM((heads, 8, tokens), f32),
+            pltpu.VMEM((heads, 8, tokens), f32),
+            pltpu.VMEM((heads, head_dim // 8, 8, tokens), f32),
+            pltpu.VMEM((tokens // 4, 8, tokens), f32),
+            pltpu.VMEM((tokens // 4, 8, tokens), f32),
+            dma((3,)),
             dma((bufs, 2)),
         ],
         compiler_params=pltpu.CompilerParams(vmem_limit_bytes=VMEM_LIMIT),
@@ -458,26 +519,38 @@
             pltpu.make_async_copy(wd_hbm.at[layer, sl, :], wd.at[slot], w_sem.at[slot, 2]),
         )
 
-    for j in range(parts):
-        o_copy(j).start()
-    for i in range(min(bufs, steps)):
-        for copy in w_copies(i, i):
-            copy.start()
+    queue = [[o_copy(j)] for j in range(parts)]
+    for i in range(min(bufs - 1, steps)):
+        queue += [[copy] for copy in w_copies(i, i)]
+    for item in queue[:3]:
+        item[0].start()
+    queue = queue[3:]
 
     for j in range(parts):
         o_copy(j).wait()
+        for item in queue[:2]:
+            item[0].start()
+        queue = queue[2:]
         sl = slice(j * o_cols, (j + 1) * o_cols)
         r = jnp.dot(o_ref[...], wo[j], preferred_element_type=jnp.float32)
         h = (h_ref[:, sl].astype(jnp.float32) + r).astype(jnp.bfloat16)
         hm[:, sl] = h
         acc[:, sl] = h.astype(jnp.float32)
-    norm_rows(hm, g_ref, nb)
+    for item in queue:
+        item[0].start()
+    norm_rows(hm, g_ref[layer:layer + 1, :], nb)
 
     @pl.loop(0, steps)
     def _(i):
         slot = lax.rem(i, bufs)
         for copy in w_copies(i, slot):
             copy.wait()
+
+        @pl.when(i + bufs - 1 < steps)
+        def _():
+            for copy in w_copies(i + bufs - 1, lax.rem(i + bufs - 1, bufs)):
+                copy.start()
+
         n = nb[...]
         for s in range(cols // sub):
             sl = slice(s * sub, (s + 1) * sub)
@@ -488,11 +561,6 @@
         for t in range(depth // span):
             sl = slice(t * span, (t + 1) * span)
             acc[:, sl] += jnp.dot(m, wd[slot, :, sl], preferred_element_type=jnp.float32)
-
-        @pl.when(i + bufs < steps)
-        def _():
-            for copy in w_copies(i + bufs, slot):
-                copy.start()
 
     out_ref[...] = acc[...].astype(jnp.bfloat16)
 
@@ -542,11 +610,11 @@
         wq = w_q.transpose(0, 2, 1, 3)
         wo = w_o.reshape(w_o.shape[0], -1, depth)
         k_all, v_all, o = gather_attend(
-            n_sp, x, g_kv.reshape(1, -1), g_attn[0:1], wk, wv, wq)
-        h = tail(0, o, x, g_mlp[0:1], wo, w_gate, w_up, w_down)
+            n_sp, x, g_kv, g_attn, wk, wv, wq)
+        h = tail(0, o, x, g_mlp, wo, w_gate, w_up, w_down)
         for layer in range(1, w_q.shape[0]):
-            o = attend(n_sp, layer, h, g_attn[layer:layer + 1], wq, k_all, v_all)
-            h = tail(layer, o, h, g_mlp[layer:layer + 1], wo, w_gate, w_up, w_down)
+            o = attend(n_sp, layer, h, g_attn, wq, k_all, v_all)
+            h = tail(layer, o, h, g_mlp, wo, w_gate, w_up, w_down)
         return h
 
     return jax.shard_map(local_block, mesh=mesh, in_specs=in_specs, out_specs=row_spec, check_vma=False)

time: 319 us -> 263 us (0.82)
  the two profiles are of different devices: /device:TPU:254 before, /device:TPU:214 now
where the time goes in v2:
time: 263 us; the launch traced here: 262 us
  Pallas kernels  262 us (100%)
    pallas_call x1, Pallas kernels, gather_attend(): pl.pallas_call(functools.partial(gather_attend_kernel, n_sp), out_shape=(...  133 us
    pallas_call x2, Pallas kernels, tail(): pl.pallas_call(functools.partial(tail_kernel, layer), out_shape=jax.Shape...  83.7 us
    pallas_call x1, Pallas kernels, attend(): pl.pallas_call(functools.partial(attend_kernel, n_sp, layer), out_shape=j...  45.5 us

profile of v2, /device:TPU:214, one launch (start us, length us, event | category | flops | bytes accessed | tf_op | source)
XLA Modules:
  0.0 262.3 jit_solution(11047823910619992955)
XLA Ops:
  0.0 133.0 %gather_attend.1 = (bf16[8,2,20,256,128]{4,3,2,1,0:T(8,128)(2,1)}, bf16[8,2,20,128,256]{4,3,2,1,0:T(8,128)(2,1)}, bf16[256,2560]{1,0:T(8,128)(2,1)}) custom-call(bf16[256,2560]{1,0:T(8,128)(2,1)} %h_ref.1, bf16[2560]{0:T(1024)(128)(2,1)} %g_kv.1, bf16[2,2560]{1,0:T(2,128)(2,1)} %g_q.3, bf16[20,2560,128]{2,1,0:T(8,128)(2,1)} %bitcast.8, ...), custom_call_target="tpu_custom_call" | custom-call | tf_op jit(solution)/shard_map/gather_attend/pallas_call | solution.py:344
  133.0 41.9 %tail.2.h_ref = bf16[256,2560]{1,0:T(8,128)(2,1)} custom-call(bf16[256,2560]{1,0:T(8,128)(2,1)} %get-tuple-element.8.o_ref, bf16[256,2560]{1,0:T(8,128)(2,1)} %h_ref.1, bf16[2,2560]{1,0:T(2,128)(2,1)} %g_ref.3, bf16[2,2560,2560]{2,1,0:T(8,128)(2,1)} %bitcast.4, bf16[2,2560,6912]{2,1,0:T(8,128)(2,1)} %wg_hbm.3, bf16[2,2560,6912]{2,1,0:T(8,128)(2,1)} %wu_hbm.3, ...), custom_call_target="tpu_custom_call" | custom-call | tf_op jit(solution)/shard_map/tail/pallas_call | solution.py:579
  174.9 45.5 %attend.1.o_ref = bf16[256,2560]{1,0:T(8,128)(2,1)} custom-call(bf16[256,2560]{1,0:T(8,128)(2,1)} %tail.2.h_ref, bf16[2,2560]{1,0:T(2,128)(2,1)} %g_q.3, bf16[2,20,2560,128]{3,2,1,0:T(8,128)(2,1)} %bitcast.7, bf16[8,2,20,256,128]{4,3,2,1,0:T(8,128)(2,1)} %get-tuple-element.9.k_all, bf16[8,2,20,128,256]{4,3,2,1,0:T(8,128)(2,1)} %get-tuple-element.10.v_all), custom_call_target="tpu_custom_call" | custom-call | tf_op jit(solution)/shard_map/attend/pallas_call | solution.py:475
  220.3 41.8 %tail.3 = bf16[256,2560]{1,0:T(8,128)(2,1)} custom-call(bf16[256,2560]{1,0:T(8,128)(2,1)} %attend.1.o_ref, bf16[256,2560]{1,0:T(8,128)(2,1)} %tail.2.h_ref, bf16[2,2560]{1,0:T(2,128)(2,1)} %g_ref.3, bf16[2,2560,2560]{2,1,0:T(8,128)(2,1)} %bitcast.5, bf16[2,2560,6912]{2,1,0:T(8,128)(2,1)} %wg_hbm.3, bf16[2,2560,6912]{2,1,0:T(8,128)(2,1)} %wu_hbm.3, ...), custom_call_target="tpu_custom_call" | custom-call | tf_op jit(solution)/shard_map/tail/pallas_call | solution.py:579

commit v3 on v2

v3 whole, which is shorter than its diff:
```python
import functools
import math

import jax
import jax.numpy as jnp
from jax import lax
from jax.experimental import pallas as pl
from jax.experimental.pallas import tpu as pltpu
from jax.sharding import PartitionSpec as P

EPS = 1e-6
LOG2E = 1.4426950408889634
MESH = pl.DeviceIdType.MESH
VMEM_LIMIT = 67043328
GROUP = 4


def norm_rows(src, gain, dst):
    rows = src.shape[0]
    step = math.gcd(rows, 16)
    g = gain.astype(jnp.float32)

    def body(i, carry):
        sl = pl.ds(pl.multiple_of(i * step, step), step)
        v = src[sl, :].astype(jnp.float32)
        inv = lax.rsqrt(jnp.mean(v * v, axis=-1, keepdims=True) + EPS)
        dst[sl, :] = (v * inv * g).astype(jnp.bfloat16)
        return carry

    lax.fori_loop(0, rows // step, body, 0, unroll=4)


def heads_matrix(w):
    return jnp.concatenate([w[i] for i in range(GROUP)], axis=1)


def project(n, w):
    return jnp.dot(n, heads_matrix(w), preferred_element_type=jnp.float32).astype(jnp.bfloat16)


def all_sublanes(x, op):
    for shift in (4, 2, 1):
        x = op(x, pltpu.roll(x, shift, 0))
    return x


def attend_block(ks, vs, q_ref, m_ref, l_ref, acc_ref, s_refs, masks=None, unroll=4):
    heads, size, head_dim = ks[0].shape
    tokens = q_ref.shape[2]
    scale = LOG2E * head_dim ** -0.5
    n = size // 8

    def scores(h, s_ref):
        top = None
        for i, k in enumerate(ks):
            s = jnp.dot(k[h], q_ref[h], preferred_element_type=jnp.float32)
            if masks is not None:
                s = jnp.where(masks[i], s, -jnp.inf)
            s = s.reshape(n, 8, tokens)
            s_ref[i * n:(i + 1) * n] = s
            t = jnp.max(s, axis=0)
            top = t if top is None else jnp.maximum(top, t)
        return all_sublanes(top, jnp.maximum)

    def update(h, s_ref, top):
        m_old = m_ref[h]
        m_new = jnp.maximum(m_old, top * scale)
        alpha = jnp.exp2(m_old - m_new)
        m_ref[h] = m_new
        p = jnp.exp2(s_ref[:n * len(ks)] * scale - m_new[None])
        l_ref[h] = l_ref[h] * alpha + jnp.sum(p, axis=0)
        p = p.reshape(size * len(ks), tokens).astype(jnp.bfloat16)
        v = jnp.concatenate([r[h] for r in vs], axis=1) if len(vs) > 1 else vs[0][h]
        o = jnp.dot(v, p, preferred_element_type=jnp.float32)
        acc_ref[h] = acc_ref[h] * alpha[None] + o.reshape(head_dim // 8, 8, tokens)

    unroll = math.gcd(heads, unroll)

    def body(g, top):
        h = unroll * g
        for i in range(unroll):
            nxt = h + i + 1
            if i == unroll - 1:
                nxt = jnp.minimum(nxt, heads - 1)
            after = scores(nxt, s_refs[(i + 1) % 2])
            update(h + i, s_refs[i % 2], top)
            top = after
        return top

    lax.fori_loop(0, heads // unroll, body, scores(0, s_refs[0]))


def reset_state(m_ref, l_ref, acc_ref):
    m_ref[...] = jnp.full_like(m_ref, -jnp.inf)
    l_ref[...] = jnp.zeros_like(l_ref)

    @pl.loop(0, acc_ref.shape[0])
    def _(h):
        acc_ref[h] = jnp.zeros(acc_ref.shape[1:], jnp.float32)


def write_attention(o_ref, l_ref, acc_ref):
    heads, _, _, tokens = acc_ref.shape
    head_dim = o_ref.shape[1] // heads

    @pl.loop(0, heads)
    def _(h):
        inv = 1.0 / all_sublanes(l_ref[h], jnp.add)
        o = (acc_ref[h] * inv[None]).reshape(head_dim, tokens)
        cols = pl.ds(pl.multiple_of(h * head_dim, head_dim), head_dim)
        o_ref[:, cols] = o.astype(jnp.bfloat16).T


def causal_mask(tokens, half, core, d):
    shape = (2 * half, tokens)
    k = lax.broadcasted_iota(jnp.int32, shape, 0)
    q = lax.broadcasted_iota(jnp.int32, shape, 1)
    key_pos = jnp.where(k >= half, k - half + tokens, k) + d * half
    return key_pos <= q + core * tokens


def attend_valid(u, chip, chips, ks, vs, state):
    s = (u + 1) // 2

    @pl.when(chip + s >= chips)
    def _():
        attend_block(ks, vs, *state, unroll=10)

    @pl.when(jnp.logical_and(chip >= s, chip + s < chips))
    def _():
        attend_block(ks[:1], vs[:1], *state)


def gather_attend_kernel(
    n_sp, x_hbm, g_kv, g_q, wk_hbm, wv_hbm, wq_hbm,
    k_all, v_all, o_ref,
    wk, wv, wq, xs, nb, kb, vb, ka, va, qt, m_ref, l_ref, acc, s0, s1,
    x_sem, w_sem, q_sem, send_sem, recv_sem, st_sem, px_sem, pr_sem, ld_sem,
):
    heads, depth, head_dim = wk.shape
    tokens = nb.shape[0]
    half = tokens // 2
    groups = heads // GROUP
    chips = n_sp // 2
    me = lax.axis_index("sp")
    chip = me // 2
    core = me - 2 * chip
    right = lax.rem(me + 2, n_sp)
    left = lax.rem(me + n_sp - 2, n_sp)
    partner = me + 1 - 2 * core

    barrier = pltpu.get_barrier_semaphore()
    for dev in (left, right, partner):
        pl.semaphore_signal(barrier, inc=1, device_id={"sp": dev}, device_id_type=MESH)
    pl.semaphore_wait(barrier, 3)

    def hop(src, u, d):
        return pltpu.make_async_remote_copy(
            src_ref=src,
            dst_ref=xs.at[u, pl.ds(d * half, half), :],
            send_sem=send_sem.at[u, d],
            recv_sem=recv_sem.at[u, d],
            device_id={"sp": right if d == 0 else left},
            device_id_type=MESH,
        )

    def own(u, d):
        return hop(x_hbm.at[pl.ds((u - 1) * half, half), :], u, d)

    def relay(u_from, u, d):
        return hop(xs.at[u_from, pl.ds(d * half, half), :], u, d)

    for u in (1, 2):
        for d in (0, 1):
            own(u, d).start()
    x_copy = pltpu.make_async_copy(x_hbm, xs.at[0], x_sem)
    x_copy.start()

    def w_copy(which, j):
        src, dst = ((wk_hbm, wk), (wv_hbm, wv))[which]
        sl = pl.ds(j * GROUP, GROUP)
        return pltpu.make_async_copy(src.at[sl], dst.at[sl], w_sem.at[which, j])

    def q_copy(j, slot):
        return pltpu.make_async_copy(
            wq_hbm.at[0, pl.ds(j * GROUP, GROUP)], wq.at[slot], q_sem.at[slot])

    ahead = min(2, groups)
    for j in range(ahead):
        w_copy(0, j).start()
        w_copy(1, j).start()
    reset_state(m_ref, l_ref, acc)
    x_copy.wait()

    cuts = [0, (groups + 1) // 2 * GROUP, heads]

    def stores(u, slot, j):
        out = []
        hs = pl.ds(cuts[j], cuts[j + 1] - cuts[j])
        for i, (buf, full) in enumerate(((kb, k_all), (vb, v_all))):
            for d in (0, 1):
                part = pl.ds(d * half, half)
                mine = pl.ds(core * half, half)
                if i == 0:
                    src, dst = buf.at[slot, hs, part, :], full.at[u, d, hs, mine, :]
                else:
                    src, dst = buf.at[slot, hs, :, part], full.at[u, d, hs, :, mine]
                local = pltpu.make_async_copy(src, dst, st_sem.at[slot, j, i, d])
                remote = pltpu.make_async_remote_copy(
                    src_ref=src, dst_ref=dst,
                    send_sem=px_sem.at[slot, j, i, d], recv_sem=pr_sem.at[u, j, i, d],
                    device_id={"sp": partner}, device_id_type=MESH,
                )
                out.append((local, remote))
        return out

    def loads(u):
        out = []
        for d in (0, 1):
            out.append(pltpu.make_async_copy(k_all.at[u, d], ka.at[d], ld_sem.at[d, 0]))
            out.append(pltpu.make_async_copy(v_all.at[u, d], va.at[d], ld_sem.at[d, 1]))
        return out

    def finish_stores(u):
        for j in (0, 1):
            for local, remote in stores(u, lax.rem(u, 2), j):
                local.wait()
                remote.wait_send()
                remote.wait_recv()

    state = (qt, m_ref, l_ref, acc, (s0, s1))

    def attend_unit(u):
        for copy in loads(u):
            copy.wait()
        attend_valid(u, chip, chips, [ka.at[0], ka.at[1]], [va.at[0], va.at[1]], state)

    def attend_own():
        for copy in loads(0):
            copy.wait()
        masks = [causal_mask(tokens, half, core, d) for d in (0, 1)]
        attend_block([ka.at[0], ka.at[1]], [va.at[0], va.at[1]], *state, masks=masks)

    def start_stores(u, slot, j):
        for local, remote in stores(u, slot, j):
            local.start()
            remote.start()

    def make_kv(slot, j):
        sl = pl.ds(j * GROUP, GROUP)
        n = nb[...]
        k = project(n, wk[sl])
        v = project(n, wv[sl])
        for i in range(GROUP):
            cols = slice(i * head_dim, (i + 1) * head_dim)
            kb[slot, j * GROUP + i] = k[:, cols]
            vb[slot, j * GROUP + i] = v[:, cols].T

    norm_rows(xs.at[0], g_kv[...].reshape(1, depth), nb)

    @pl.loop(0, groups)
    def _(j):
        w_copy(0, j).wait()
        w_copy(1, j).wait()

        @pl.when(j + ahead < groups)
        def _():
            w_copy(0, j + ahead).start()
            w_copy(1, j + ahead).start()

        @pl.when(j + ahead >= groups)
        def _():
            q_copy(j + ahead - groups, j + ahead - groups).start()

        make_kv(0, j)

    for j in (0, 1):
        start_stores(0, 0, j)
    norm_rows(xs.at[0], g_q[0:1, :], nb)

    @pl.loop(0, groups)
    def _(j):
        qslot = lax.rem(j, 2)
        q_copy(j, qslot).wait()
        q = project(nb[...], wq[qslot])
        for i in range(GROUP):
            qt[j * GROUP + i] = q[:, i * head_dim:(i + 1) * head_dim].T

        @pl.when(j + 2 < groups)
        def _():
            q_copy(j + 2, qslot).start()

    @pl.loop(1, chips + 1)
    def _(u):
        @pl.when(u < chips)
        def _():
            for d in (0, 1):
                relay(0, u, d).wait_recv()

        @pl.when(u <= chips - 4)
        def _():
            for d in (0, 1):
                relay(u, u + 2, d).start()

        @pl.when(u == chips - 3)
        def _():
            relay(u, u + 2, 0).start()

        @pl.when(u == chips - 2)
        def _():
            relay(u, u + 1, 1).start()

        finish_stores(u - 1)
        for copy in loads(u - 1):
            copy.start()

        @pl.when(u < chips)
        def _():
            norm_rows(xs.at[u], g_kv[...].reshape(1, depth), nb)
            for j in range(groups):
                make_kv(lax.rem(u, 2), j)
                for i in (0, 1):
                    if (j + 1) * GROUP == cuts[i + 1]:
                        start_stores(u, lax.rem(u, 2), i)

        @pl.when(u == 1)
        def _():
            attend_own()

        @pl.when(u >= 2)
        def _():
            attend_unit(u - 1)

    write_attention(o_ref, l_ref, acc)
    for u in range(1, chips):
        for d in (0, 1):
            relay(0, u, d).wait_send()


def gather_attend(n_sp, x, g_kv, g_q, wk, wv, wq):
    tokens, depth = x.shape
    heads, _, head_dim = wk.shape
    chips = n_sp // 2
    bf, f32 = jnp.bfloat16, jnp.float32
    dma = pltpu.SemaphoreType.DMA
    groups = heads // GROUP
    any_spec = pl.BlockSpec(memory_space=pl.ANY)
    vmem = pl.BlockSpec(memory_space=pltpu.VMEM)
    return pl.pallas_call(
        functools.partial(gather_attend_kernel, n_sp),
        out_shape=(
            jax.ShapeDtypeStruct((chips, 2, heads, tokens, head_dim), bf),
            jax.ShapeDtypeStruct((chips, 2, heads, head_dim, tokens), bf),
            jax.ShapeDtypeStruct((tokens, heads * head_dim), bf),
        ),
        in_specs=[any_spec, vmem, vmem, any_spec, any_spec, any_spec],
        out_specs=(any_spec, any_spec, vmem),
        scratch_shapes=[
            pltpu.VMEM((heads, depth, head_dim), bf),
            pltpu.VMEM((heads, depth, head_dim), bf),
            pltpu.VMEM((2, GROUP, depth, head_dim), bf),
            pltpu.VMEM((chips, tokens, depth), bf),
            pltpu.VMEM((tokens, depth), bf),
            pltpu.VMEM((2, heads, tokens, head_dim), bf),
            pltpu.VMEM((2, heads, head_dim, tokens), bf),
            pltpu.VMEM((2, heads, tokens, head_dim), bf),
            pltpu.VMEM((2, heads, head_dim, tokens), bf),
            pltpu.VMEM((heads, head_dim, tokens), bf),
            pltpu.VMEM((heads, 8, tokens), f32),
            pltpu.VMEM((heads, 8, tokens), f32),
            pltpu.VMEM((heads, head_dim // 8, 8, tokens), f32),
            pltpu.VMEM((tokens // 4, 8, tokens), f32),
            pltpu.VMEM((tokens // 4, 8, tokens), f32),
            dma,
            dma((2, groups)),
            dma((2,)),
            dma((chips, 2)),
            dma((chips, 2)),
            dma((2, 2, 2, 2)),
            dma((2, 2, 2, 2)),
            dma((chips, 2, 2, 2)),
            dma((2, 2)),
        ],
        compiler_params=pltpu.CompilerParams(
            collective_id=0, has_side_effects=True, vmem_limit_bytes=VMEM_LIMIT
        ),
        name="gather_attend",
    )(x, g_kv, g_q, wk, wv, wq)


def rest_kernel(
    n_sp, o_hbm, x_hbm, g_attn, g_mlp, wq_hbm, wo_hbm, wg_hbm, wu_hbm, wd_hbm, k_all, v_all,
    h_ref,
    wb, wg, wu, wd, ka, va, qt, m_ref, l_ref, acc, s0, s1, ob, nb, sums, mb,
    b_sem, w_sem, ld_sem, in_sem,
):
    layers, heads, depth, head_dim = wq_hbm.shape
    tokens = nb.shape[0]
    half = tokens // 2
    groups = heads // GROUP
    chips = n_sp // 2
    blocks = depth // head_dim
    cols = wg.shape[2]
    steps = wg_hbm.shape[2] // cols
    sub = math.gcd(cols, 256)
    span = math.gcd(depth, 512)
    me = lax.axis_index("sp")
    chip = me // 2
    core = me - 2 * chip

    def q_copy(layer, j):
        return pltpu.make_async_copy(wq_hbm.at[layer, j], wb.at[j], b_sem.at[j])

    def o_copy(layer, j):
        return pltpu.make_async_copy(
            wo_hbm.at[layer, :, pl.ds(j * head_dim, head_dim)], wb.at[j], b_sem.at[j])

    def w_copies(layer, i, slot):
        sl = pl.ds(pl.multiple_of(i * cols, cols), cols)
        return (
            pltpu.make_async_copy(wg_hbm.at[layer, :, sl], wg.at[slot], w_sem.at[slot, 0]),
            pltpu.make_async_copy(wu_hbm.at[layer, :, sl], wu.at[slot], w_sem.at[slot, 1]),
            pltpu.make_async_copy(wd_hbm.at[layer, sl, :], wd.at[slot], w_sem.at[slot, 2]),
        )

    def loads(u, slot):
        return (
            pltpu.make_async_copy(k_all.at[u], ka.at[slot], ld_sem.at[slot, 0]),
            pltpu.make_async_copy(v_all.at[u], va.at[slot], ld_sem.at[slot, 1]),
        )

    def output_projection(layer, queue):
        for j in range(blocks // GROUP):
            for i in range(GROUP):
                o_copy(layer, j * GROUP + i).wait()
            for copy in queue[j * GROUP:(j + 1) * GROUP]:
                copy.start()
            sl = slice(j * GROUP * head_dim, (j + 1) * GROUP * head_dim)
            w = heads_matrix(wb[j * GROUP:(j + 1) * GROUP])
            r = jnp.dot(ob[...], w, preferred_element_type=jnp.float32)
            h = (h_ref[:, sl].astype(jnp.float32) + r).astype(jnp.bfloat16)
            h_ref[:, sl] = h
            sums[:, sl] = h.astype(jnp.float32)

    def mlp(layer):
        norm_rows(h_ref, g_mlp[layer:layer + 1, :], nb)

        @pl.loop(0, steps)
        def _(i):
            slot = lax.rem(i, 2)
            for copy in w_copies(layer, i, slot):
                copy.wait()
            n = nb[...]
            for s in range(cols // sub):
                sl = slice(s * sub, (s + 1) * sub)
                a = jnp.dot(n, wg[slot, :, sl], preferred_element_type=jnp.float32)
                b = jnp.dot(n, wu[slot, :, sl], preferred_element_type=jnp.float32)
                mb[:, sl] = (jax.nn.silu(a) * b).astype(jnp.bfloat16)

            @pl.when(i + 2 < steps)
            def _():
                for copy in w_copies(layer, i + 2, slot)[:2]:
                    copy.start()

            if layer + 1 < layers:
                @pl.when(i == steps - 2)
                def _():
                    for j in range(heads):
                        q_copy(layer + 1, j).start()

                @pl.when(i == steps - 1)
                def _():
                    for u in (0, 1):
                        for copy in loads(u, u):
                            copy.start()

            m = mb[...]
            for t in range(depth // span):
                sl = slice(t * span, (t + 1) * span)
                sums[:, sl] += jnp.dot(m, wd[slot, :, sl], preferred_element_type=jnp.float32)

            @pl.when(i + 2 < steps)
            def _():
                w_copies(layer, i + 2, slot)[2].start()

        h_ref[...] = sums[...].astype(jnp.bfloat16)

    def attention(layer):
        norm_rows(h_ref, g_attn[layer:layer + 1, :], nb)
        reset_state(m_ref, l_ref, acc)
        for j in range(heads):
            q_copy(layer, j).wait()
        for j in range(groups):
            q = project(nb[...], wb[j * GROUP:(j + 1) * GROUP])
            for i in range(GROUP):
                qt[j * GROUP + i] = q[:, i * head_dim:(i + 1) * head_dim].T

        state = (qt, m_ref, l_ref, acc, (s0, s1))
        first = w_copies(layer, 0, 0)
        second = w_copies(layer, 1, 1)
        ahead = [[o_copy(layer, j) for j in range(blocks)], [], first[:2], first[2:],
                 second[:1], second[1:2], second[2:]]

        @pl.loop(0, chips)
        def _(u):
            slot = lax.rem(u, 2)
            for copy in loads(u, slot):
                copy.wait()
            for i, copies in enumerate(ahead):
                if copies:
                    @pl.when(u == i)
                    def _(copies=copies):
                        for copy in copies:
                            copy.start()

            ks = [ka.at[slot, d] for d in (0, 1)]
            vs = [va.at[slot, d] for d in (0, 1)]

            @pl.when(u == 0)
            def _():
                masks = [causal_mask(tokens, half, core, d) for d in (0, 1)]
                attend_block(ks, vs, *state, masks=masks)

            @pl.when(u > 0)
            def _():
                attend_valid(u, chip, chips, ks, vs, state)

            @pl.when(u + 2 < chips)
            def _():
                for copy in loads(u + 2, slot):
                    copy.start()

        write_attention(ob, l_ref, acc)

    inputs = (pltpu.make_async_copy(o_hbm, ob, in_sem.at[0]),
              pltpu.make_async_copy(x_hbm, h_ref, in_sem.at[1]))
    for copy in inputs:
        copy.start()
    queue = [o_copy(0, j) for j in range(blocks)]
    for copy in queue[:2 * GROUP]:
        copy.start()
    first = w_copies(0, 0, 0)
    second = w_copies(0, 1, 1)
    queue = queue[2 * GROUP:]
    queue += [*first, *second]
    for copy in inputs:
        copy.wait()
    output_projection(0, queue)
    for copy in queue[blocks:]:
        copy.start()
    mlp(0)
    for layer in range(1, layers):
        attention(layer)
        output_projection(layer, [])
        mlp(layer)


def rest(n_sp, o, x, g_attn, g_mlp, wq, wo, wg, wu, wd, k_all, v_all):
    tokens, depth = x.shape
    _, heads, _, head_dim = wq.shape
    bf, f32 = jnp.bfloat16, jnp.float32
    dma = pltpu.SemaphoreType.DMA
    cols = math.gcd(wg.shape[2], 768)
    any_spec = pl.BlockSpec(memory_space=pl.ANY)
    vmem = pl.BlockSpec(memory_space=pltpu.VMEM)
    return pl.pallas_call(
        functools.partial(rest_kernel, n_sp),
        out_shape=jax.ShapeDtypeStruct((tokens, depth), bf),
        in_specs=[any_spec, any_spec, vmem, vmem] + [any_spec] * 7,
        out_specs=vmem,
        scratch_shapes=[
            pltpu.VMEM((max(heads, depth // head_dim), depth, head_dim), bf),
            pltpu.VMEM((2, depth, cols), bf),
            pltpu.VMEM((2, depth, cols), bf),
            pltpu.VMEM((2, cols, depth), bf),
            pltpu.VMEM((2, 2, heads, tokens, head_dim), bf),
            pltpu.VMEM((2, 2, heads, head_dim, tokens), bf),
            pltpu.VMEM((heads, head_dim, tokens), bf),
            pltpu.VMEM((heads, 8, tokens), f32),
            pltpu.VMEM((heads, 8, tokens), f32),
            pltpu.VMEM((heads, head_dim // 8, 8, tokens), f32),
            pltpu.VMEM((tokens // 4, 8, tokens), f32),
            pltpu.VMEM((tokens // 4, 8, tokens), f32),
            pltpu.VMEM((tokens, heads * head_dim), bf),
            pltpu.VMEM((tokens, depth), bf),
            pltpu.VMEM((tokens, depth), f32),
            pltpu.VMEM((tokens, cols), bf),
            dma((max(heads, depth // head_dim),)),
            dma((2, 3)),
            dma((2, 2)),
            dma((2,)),
        ],
        compiler_params=pltpu.CompilerParams(vmem_limit_bytes=VMEM_LIMIT),
        name="rest",
    )(o, x, g_attn, g_mlp, wq, wo, wg, wu, wd, k_all, v_all)


def solution(mesh):
    n_sp = mesh.shape["sp"]
    row_spec = P(("dp", "sp"), None)
    in_specs = (row_spec,) + (P(),) * 10

    def local_block(x, g_kv, w_k, w_v, g_attn, w_q, w_o, g_mlp, w_gate, w_up, w_down):
        depth = x.shape[1]
        wk = w_k.transpose(1, 0, 2)
        wv = w_v.transpose(1, 0, 2)
        wq = w_q.transpose(0, 2, 1, 3)
        wo = w_o.reshape(w_o.shape[0], -1, depth)
        k_all, v_all, o = gather_attend(
            n_sp, x, g_kv, g_attn, wk, wv, wq)
        h = rest(n_sp, o, x, g_attn, g_mlp, wq, wo, w_gate, w_up, w_down, k_all, v_all)
        return h

    return jax.shard_map(local_block, mesh=mesh, in_specs=in_specs, out_specs=row_spec, check_vma=False)
```

time: 263 us -> 248 us (0.943)
  the two profiles are of different devices: /device:TPU:214 before, /device:TPU:246 now
where the time goes in v3:
time: 248 us
  Pallas kernels  248 us (100%)
    pallas_call x1, Pallas kernels, gather_attend(): pl.pallas_call(functools.partial(gather_attend_kernel, n_sp), out_shape=(...  127 us
    pallas_call x1, Pallas kernels, rest(): pl.pallas_call(functools.partial(rest_kernel, n_sp), out_shape=jax.ShapeD...  121 us

profile of v3, /device:TPU:246, one launch (start us, length us, event | category | flops | bytes accessed | tf_op | source)
XLA Modules:
  0.0 248.0 jit_solution(9835368836670284901)
XLA Ops:
  0.0 126.7 %gather_attend.1 = (bf16[8,2,20,256,128]{4,3,2,1,0:T(8,128)(2,1)}, bf16[8,2,20,128,256]{4,3,2,1,0:T(8,128)(2,1)}, bf16[256,2560]{1,0:T(8,128)(2,1)}) custom-call(bf16[256,2560]{1,0:T(8,128)(2,1)} %x_hbm.3, bf16[2560]{0:T(1024)(128)(2,1)} %g_kv.1, bf16[2,2560]{1,0:T(2,128)(2,1)} %g_attn.1, bf16[20,2560,128]{2,1,0:T(8,128)(2,1)} %bitcast.7, ...), custom_call_target="tpu_custom_call" | custom-call | tf_op jit(solution)/shard_map/gather_attend/pallas_call | solution.py:349
  126.7 121.1 %rest.1 = bf16[256,2560]{1,0:T(8,128)(2,1)} custom-call(bf16[256,2560]{1,0:T(8,128)(2,1)} %get-tuple-element.8.o_hbm, bf16[256,2560]{1,0:T(8,128)(2,1)} %x_hbm.3, bf16[2,2560]{1,0:T(2,128)(2,1)} %g_attn.1, bf16[2,2560]{1,0:T(2,128)(2,1)} %g_mlp.1, bf16[2,20,2560,128]{3,2,1,0:T(8,128)(2,1)} %bitcast.5, bf16[2,2560,2560]{2,1,0:T(8,128)(2,1)} %bitcast.6, ...), custom_call_target="tpu_custom_call" | custom-call | tf_op jit(solution)/shard_map/rest/pallas_call | solution.py:566

commit v4 on v3

--- a/solution.py
+++ b/solution.py
@@ -15,6 +15,9 @@
 GROUP = 4
 
 
+SLOTS = 5
+
+
 def norm_rows(src, gain, dst):
     rows = src.shape[0]
     step = math.gcd(rows, 16)
@@ -44,7 +47,7 @@
     return x
 
 
-def attend_block(ks, vs, q_ref, m_ref, l_ref, acc_ref, s_refs, masks=None, unroll=4):
+def attend_block(ks, vs, q_ref, m_ref, l_ref, acc_ref, s_refs, masks=None, unroll=10):
     heads, size, head_dim = ks[0].shape
     tokens = q_ref.shape[2]
     scale = LOG2E * head_dim ** -0.5
@@ -75,19 +78,23 @@
         acc_ref[h] = acc_ref[h] * alpha[None] + o.reshape(head_dim // 8, 8, tokens)
 
     unroll = math.gcd(heads, unroll)
-
-    def body(g, top):
+    assert unroll % len(s_refs) == 0
+
+    depth = min(2, len(s_refs) - 1)
+
+    def body(g, tops):
         h = unroll * g
+        tops = list(tops)
         for i in range(unroll):
-            nxt = h + i + 1
-            if i == unroll - 1:
+            nxt = h + i + depth
+            if i >= unroll - depth:
                 nxt = jnp.minimum(nxt, heads - 1)
-            after = scores(nxt, s_refs[(i + 1) % 2])
-            update(h + i, s_refs[i % 2], top)
-            top = after
-        return top
-
-    lax.fori_loop(0, heads // unroll, body, scores(0, s_refs[0]))
+            tops.append(scores(nxt, s_refs[(i + depth) % len(s_refs)]))
+            update(h + i, s_refs[i % len(s_refs)], tops.pop(0))
+        return tuple(tops)
+
+    tops = tuple(scores(i, s_refs[i]) for i in range(depth))
+    lax.fori_loop(0, heads // unroll, body, tops)
 
 
 def reset_state(m_ref, l_ref, acc_ref):
@@ -103,12 +110,14 @@
     heads, _, _, tokens = acc_ref.shape
     head_dim = o_ref.shape[1] // heads
 
-    @pl.loop(0, heads)
-    def _(h):
+    def body(h, carry):
         inv = 1.0 / all_sublanes(l_ref[h], jnp.add)
         o = (acc_ref[h] * inv[None]).reshape(head_dim, tokens)
         cols = pl.ds(pl.multiple_of(h * head_dim, head_dim), head_dim)
         o_ref[:, cols] = o.astype(jnp.bfloat16).T
+        return carry
+
+    lax.fori_loop(0, heads, body, 0, unroll=4)
 
 
 def causal_mask(tokens, half, core, d):
@@ -134,7 +143,7 @@
 def gather_attend_kernel(
     n_sp, x_hbm, g_kv, g_q, wk_hbm, wv_hbm, wq_hbm,
     k_all, v_all, o_ref,
-    wk, wv, wq, xs, nb, kb, vb, ka, va, qt, m_ref, l_ref, acc, s0, s1,
+    wk, wv, wq, xs, nb, kb, vb, ka, va, qt, m_ref, l_ref, acc, s_refs,
     x_sem, w_sem, q_sem, send_sem, recv_sem, st_sem, px_sem, pr_sem, ld_sem,
 ):
     heads, depth, head_dim = wk.shape
@@ -214,11 +223,12 @@
                 out.append((local, remote))
         return out
 
-    def loads(u):
+    def loads(u, j):
+        hs = pl.ds(cuts[j], cuts[j + 1] - cuts[j])
         out = []
         for d in (0, 1):
-            out.append(pltpu.make_async_copy(k_all.at[u, d], ka.at[d], ld_sem.at[d, 0]))
-            out.append(pltpu.make_async_copy(v_all.at[u, d], va.at[d], ld_sem.at[d, 1]))
+            out.append(pltpu.make_async_copy(k_all.at[u, d, hs], ka.at[d, hs], ld_sem.at[d, 0, j]))
+            out.append(pltpu.make_async_copy(v_all.at[u, d, hs], va.at[d, hs], ld_sem.at[d, 1, j]))
         return out
 
     def finish_stores(u):
@@ -227,17 +237,22 @@
                 local.wait()
                 remote.wait_send()
                 remote.wait_recv()
-
-    state = (qt, m_ref, l_ref, acc, (s0, s1))
+            for copy in loads(u, j):
+                copy.start()
+
+    def wait_loads(u):
+        for j in (0, 1):
+            for copy in loads(u, j):
+                copy.wait()
+
+    state = (qt, m_ref, l_ref, acc, [s_refs.at[i] for i in range(s_refs.shape[0])])
 
     def attend_unit(u):
-        for copy in loads(u):
-            copy.wait()
+        wait_loads(u)
         attend_valid(u, chip, chips, [ka.at[0], ka.at[1]], [va.at[0], va.at[1]], state)
 
     def attend_own():
-        for copy in loads(0):
-            copy.wait()
+        wait_loads(0)
         masks = [causal_mask(tokens, half, core, d) for d in (0, 1)]
         attend_block([ka.at[0], ka.at[1]], [va.at[0], va.at[1]], *state, masks=masks)
 
@@ -311,8 +326,6 @@
             relay(u, u + 1, 1).start()
 
         finish_stores(u - 1)
-        for copy in loads(u - 1):
-            copy.start()
 
         @pl.when(u < chips)
         def _():
@@ -369,8 +382,7 @@
             pltpu.VMEM((heads, 8, tokens), f32),
             pltpu.VMEM((heads, 8, tokens), f32),
             pltpu.VMEM((heads, head_dim // 8, 8, tokens), f32),
-            pltpu.VMEM((tokens // 4, 8, tokens), f32),
-            pltpu.VMEM((tokens // 4, 8, tokens), f32),
+            pltpu.VMEM((SLOTS, tokens // 4, 8, tokens), f32),
             dma,
             dma((2, groups)),
             dma((2,)),
@@ -379,7 +391,7 @@
             dma((2, 2, 2, 2)),
             dma((2, 2, 2, 2)),
             dma((chips, 2, 2, 2)),
-            dma((2, 2)),
+            dma((2, 2, 2)),
         ],
         compiler_params=pltpu.CompilerParams(
             collective_id=0, has_side_effects=True, vmem_limit_bytes=VMEM_LIMIT
@@ -391,7 +403,7 @@
 def rest_kernel(
     n_sp, o_hbm, x_hbm, g_attn, g_mlp, wq_hbm, wo_hbm, wg_hbm, wu_hbm, wd_hbm, k_all, v_all,
     h_ref,
-    wb, wg, wu, wd, ka, va, qt, m_ref, l_ref, acc, s0, s1, ob, nb, sums, mb,
+    wb, wg, wu, wd, ka, va, qt, m_ref, l_ref, acc, s_refs, ob, nb, sums, mb,
     b_sem, w_sem, ld_sem, in_sem,
 ):
     layers, heads, depth, head_dim = wq_hbm.shape
@@ -495,7 +507,7 @@
             for i in range(GROUP):
                 qt[j * GROUP + i] = q[:, i * head_dim:(i + 1) * head_dim].T
 
-        state = (qt, m_ref, l_ref, acc, (s0, s1))
+        state = (qt, m_ref, l_ref, acc, [s_refs.at[i] for i in range(s_refs.shape[0])])
         first = w_copies(layer, 0, 0)
         second = w_copies(layer, 1, 1)
         ahead = [[o_copy(layer, j) for j in range(blocks)], [], first[:2], first[2:],
@@ -579,8 +591,7 @@
             pltpu.VMEM((heads, 8, tokens), f32),
             pltpu.VMEM((heads, 8, tokens), f32),
             pltpu.VMEM((heads, head_dim // 8, 8, tokens), f32),
-            pltpu.VMEM((tokens // 4, 8, tokens), f32),
-            pltpu.VMEM((tokens // 4, 8, tokens), f32),
+            pltpu.VMEM((SLOTS, tokens // 4, 8, tokens), f32),
             pltpu.VMEM((tokens, heads * head_dim), bf),
             pltpu.VMEM((tokens, depth), bf),
             pltpu.VMEM((tokens, depth), f32),

time: 248 us -> 237 us (0.956)
  the two profiles are of different devices: /device:TPU:246 before, /device:TPU:21 now
where the time goes in v4:
time: 237 us; the launch traced here: 232 us
  Pallas kernels  232 us (98%)
    pallas_call x1, Pallas kernels, gather_attend(): pl.pallas_call(functools.partial(gather_attend_kernel, n_sp), out_shape=(...  125 us
    pallas_call x1, Pallas kernels, rest(): pl.pallas_call(functools.partial(rest_kernel, n_sp), out_shape=jax.ShapeD...  107 us

profile of v4, /device:TPU:21, one launch (start us, length us, event | category | flops | bytes accessed | tf_op | source)
XLA Modules:
  0.0 232.4 jit_solution(16841347756496667719)
XLA Ops:
  0.0 125.2 %gather_attend.1 = (bf16[8,2,20,256,128]{4,3,2,1,0:T(8,128)(2,1)}, bf16[8,2,20,128,256]{4,3,2,1,0:T(8,128)(2,1)}, bf16[256,2560]{1,0:T(8,128)(2,1)}) custom-call(bf16[256,2560]{1,0:T(8,128)(2,1)} %x_hbm.3, bf16[2560]{0:T(1024)(128)(2,1)} %g_kv.1, bf16[2,2560]{1,0:T(2,128)(2,1)} %g_attn.1, bf16[20,2560,128]{2,1,0:T(8,128)(2,1)} %bitcast.7, ...), custom_call_target="tpu_custom_call" | custom-call | tf_op jit(solution)/shard_map/gather_attend/pallas_call | solution.py:362
  125.2 107.0 %rest.1 = bf16[256,2560]{1,0:T(8,128)(2,1)} custom-call(bf16[256,2560]{1,0:T(8,128)(2,1)} %get-tuple-element.8.o_hbm, bf16[256,2560]{1,0:T(8,128)(2,1)} %x_hbm.3, bf16[2,2560]{1,0:T(2,128)(2,1)} %g_attn.1, bf16[2,2560]{1,0:T(2,128)(2,1)} %g_mlp.1, bf16[2,20,2560,128]{3,2,1,0:T(8,128)(2,1)} %bitcast.5, bf16[2,2560,2560]{2,1,0:T(8,128)(2,1)} %bitcast.6, ...), custom_call_target="tpu_custom_call" | custom-call | tf_op jit(solution)/shard_map/rest/pallas_call | solution.py:578
